TPU v7x, 8 devices: a whole 2x2x1 slice. The times are simulated.
8 devices in a mesh: dp: 1 (over z), yax: 2 (over y), xax: 4 (over x, core).
Axes of the slice: x: 2, y: 2, z: 1, core: 2. Of those that a mesh axis runs over, the one named last changes fastest.
Arguments:
- hidden: bfloat16 [128, 4096], P('dp', 'xax')
- cache_len: int32 [128], P('dp')
- k_cache: bfloat16 [128, 8192, 128], P(('dp', 'yax', 'xax'))
- v_cache: bfloat16 [128, 8192, 128], P(('dp', 'yax', 'xax'))
- g_attn: float32 [4096], P('xax')
- w_query: bfloat16 [4096, 4096], P('xax', 'yax')
- w_key: bfloat16 [4096, 128], P('xax')
- w_value: bfloat16 [4096, 128], P('xax')
- w_gate: bfloat16 [4096, 16384], P('xax', 'yax')
- w_up: bfloat16 [4096, 16384], P('xax', 'yax')
- w_out: bfloat16 [4096, 4096], P('yax', 'xax')
- w_down: bfloat16 [16384, 4096], P('yax', 'xax')
- g_final: float32 [4096], P('xax')
- embedding: bfloat16 [50432, 4096], P('yax', 'xax')
Outputs:
- output 1: bfloat16 [128, 128], P(('dp', 'yax', 'xax'))
- output 2: bfloat16 [128, 128], P(('dp', 'yax', 'xax'))
- output 3: float32 [128, 50432], P('dp', ('yax', 'xax'))
- output 4: float32 [128], P('dp')
All inputs are finite; a program needn't handle non-finite values.
Results may differ from a plain program's by a relative error of at most 0.001.
Values are sent between devices in bfloat16 or wider.
A program may use at most 1 GiB of HBM per device.

v0:
```python
import jax
import jax.numpy as jnp
from jax import lax
from jax.sharding import PartitionSpec as P

EPS = 1e-6
ROPE_BASE = 10000.0


def rope_angle(positions, head_dim):
    half_dim = head_dim // 2
    inv_freq = ROPE_BASE ** (-(jnp.arange(half_dim, dtype=jnp.float32) * 2.0) / head_dim)
    return positions.astype(jnp.float32)[:, None] * inv_freq[None, :]


def rotary(values_in, angles):
    half_dim = values_in.shape[-1] // 2
    cos_a = jnp.cos(angles)
    sin_a = jnp.sin(angles)
    first = values_in[..., :half_dim]
    second = values_in[..., half_dim:]
    return jnp.concatenate([first * cos_a - second * sin_a, second * cos_a + first * sin_a], axis=-1)


def sharded_norm(values_in, gain, width):
    stats = jnp.stack([jnp.sum(values_in, axis=-1), jnp.sum(values_in * values_in, axis=-1)])
    stats = lax.psum(stats, "xax")
    row_mean = stats[0] / width
    row_var = stats[1] / width - row_mean * row_mean
    return (values_in - row_mean[:, None]) * lax.rsqrt(row_var + EPS)[:, None] * gain


def attend_local(query, k_cache, v_cache, key_new, value_new, lengths):
    score_scale = query.shape[-1] ** -0.5
    scores = jnp.einsum("bhe,bse->bhs", query, k_cache, preferred_element_type=jnp.float32) * score_scale
    score_new = jnp.einsum("bhe,be->bh", query, key_new, preferred_element_type=jnp.float32) * score_scale
    valid = jnp.arange(k_cache.shape[1])[None, None, :] < lengths[:, None, None]
    row_max = jnp.maximum(jnp.max(jnp.where(valid, scores, -jnp.inf), axis=-1), score_new)
    weights = jnp.where(valid, jnp.exp(scores - row_max[..., None]), 0.0)
    weight_new = jnp.exp(score_new - row_max)
    denominator = jnp.sum(weights, axis=-1) + weight_new
    prob_all = (weights / denominator[..., None]).astype(jnp.bfloat16)
    prob_new = (weight_new / denominator).astype(jnp.bfloat16)
    attn_out = jnp.einsum("bhs,bse->bhe", prob_all, v_cache, preferred_element_type=jnp.float32)
    attn_out = attn_out + prob_new.astype(jnp.float32)[..., None] * value_new.astype(jnp.float32)[:, None, :]
    return attn_out.astype(jnp.bfloat16)


def solution(mesh):
    y_size = mesh.shape["yax"]
    x_size = mesh.shape["xax"]
    row_spec = P(("dp", "yax", "xax"))

    def local_step(hidden, cache_len, k_cache, v_cache, g_attn, w_query, w_key, w_value,
                   w_gate, w_up, w_out, w_down, g_final, embedding):
        rows = hidden.shape[0]
        width = hidden.shape[1] * x_size
        own_rows = k_cache.shape[0]
        head_dim = k_cache.shape[2]
        q_cols = w_query.shape[1]
        kv_end = q_cols + 2 * head_dim
        ff_end = kv_end + w_gate.shape[1]
        y_idx = lax.axis_index("yax")
        x_idx = lax.axis_index("xax")
        own_start = (y_idx * x_size + x_idx) * own_rows

        residual = hidden.astype(jnp.float32)
        normed = sharded_norm(residual, g_attn, width).astype(jnp.bfloat16)
        proj_part = jnp.concatenate([
            jnp.dot(normed, w_query, preferred_element_type=jnp.float32),
            jnp.dot(normed, w_key, preferred_element_type=jnp.float32),
            jnp.dot(normed, w_value, preferred_element_type=jnp.float32),
            jnp.dot(normed, w_gate, preferred_element_type=jnp.float32),
            jnp.dot(normed, w_up, preferred_element_type=jnp.float32)], axis=1)
        projected = lax.psum(proj_part, "xax").astype(jnp.bfloat16)
        angles = rope_angle(cache_len, head_dim)
        query = projected[:, :q_cols].astype(jnp.float32).reshape(rows, q_cols // head_dim, head_dim)
        query = rotary(query, angles[:, None, :]).astype(jnp.bfloat16)
        key_new = rotary(projected[:, q_cols:q_cols + head_dim].astype(jnp.float32), angles).astype(jnp.bfloat16)
        value_new = projected[:, q_cols + head_dim:kv_end]
        gate = projected[:, kv_end:ff_end]
        up_val = projected[:, ff_end:]

        query_grp = lax.all_to_all(query, "yax", 0, 1, tiled=True)
        query_own = lax.dynamic_slice_in_dim(query_grp, x_idx * own_rows, own_rows, axis=0)
        key_own = lax.dynamic_slice_in_dim(key_new, own_start, own_rows, axis=0)
        value_own = lax.dynamic_slice_in_dim(value_new, own_start, own_rows, axis=0)
        len_own = lax.dynamic_slice_in_dim(cache_len, own_start, own_rows, axis=0)
        attn_own = attend_local(query_own, k_cache, v_cache, key_own, value_own, len_own)
        attn_grp = lax.all_gather(attn_own, "xax", axis=0, tiled=True)
        attn_heads = lax.all_to_all(attn_grp, "yax", 1, 0, tiled=True).reshape(rows, q_cols)

        mlp_act = (jax.nn.silu(gate.astype(jnp.float32)) * up_val.astype(jnp.float32)).astype(jnp.bfloat16)
        branch_sum = (jnp.dot(attn_heads, w_out, preferred_element_type=jnp.float32)
                      + jnp.dot(mlp_act, w_down, preferred_element_type=jnp.float32))
        residual_out = residual + lax.psum(branch_sum, "yax")
        final_norm = sharded_norm(residual_out, g_final, width).astype(jnp.bfloat16)
        logit_part = jnp.einsum("bd,vd->bv", final_norm, embedding, preferred_element_type=jnp.float32)
        logits = lax.psum_scatter(logit_part, "xax", scatter_dimension=1, tiled=True)
        row_max = lax.pmax(jnp.max(logits, axis=1), ("yax", "xax"))
        sum_exp = lax.psum(jnp.sum(jnp.exp(logits - row_max[:, None]), axis=1), ("yax", "xax"))
        log_norm = row_max + jnp.log(sum_exp)
        return key_own, value_own, logits - log_norm[:, None], log_norm

    in_specs = (P("dp", "xax"), P("dp"), row_spec, row_spec, P("xax"), P("xax", "yax"),
                P("xax", None), P("xax", None), P("xax", "yax"), P("xax", "yax"),
                P("yax", "xax"), P("yax", "xax"), P("xax"), P("yax", "xax"))
    out_specs = (row_spec, row_spec, P("dp", ("yax", "xax")), P("dp"))
    return jax.shard_map(local_step, mesh=mesh, in_specs=in_specs, out_specs=out_specs, check_vma=False)
```

profile of v0, /device:TPU:0, one launch (start us, length us, event | category | flops | bytes accessed | tf_op | source)
XLA Modules:
  0.0 512.1 jit_solution(6137129506511060863)
XLA Ops:
  8.3 8.8 %psum.35 = f32[2,128]{1,0:T(2,128)S(1)} all-reduce(f32[2,128]{1,0:T(2,128)S(1)} %pad_maximum_fusion.1), channel_id=1, replica_groups=mesh['dp'=1,'yax'=2,'xax'=4] {'xax'}, use_global_device_ids=true, to_apply=%region_2.0 | all-reduce | flops 256 | bytes 2048 | tf_op jit(solution)/shard_map/psum | solution.py:27
  17.1 4.2 convolution_dynamic-update-slice_fusion.2
  23.3 2.0 convolution_dynamic-update-slice_fusion.3
  25.2 10.5 %convolution_dynamic-update-slice_fusion.1 = f32[128,18688]{1,0:T(8,128)} fusion(f32[128,18688]{1,0:T(8,128)} %convolution_dynamic-update-slice_fusion.3, bf16[1024,8192]{1,0:T(8,128)(2,1)} %param.22, bf16[128,1024]{1,0:T(8,128)(2,1)} %param.14, f32[1024]{0:T(1024)} %param.18, f32[128]{0:T(128)S(1)} %fusion.39, f32[128]{0:T(128)S(1)} %multiply_bitcast_fusion.1), kind=kOutput, calls=%fused_computation.5 | convolution fusion | flops 2148139008 | bytes 21238784 | tf_op jit(solution)/shard_map/dot_general | solution.py:73
  35.8 4.5 convolution_dynamic-update-slice_fusion
  40.2 166.1 %all-reduce.4 = bf16[128,18688]{1,0:T(8,128)(2,1)} all-reduce(f32[128,18688]{1,0:T(8,128)} %convolution_dynamic-update-slice_fusion), channel_id=1, replica_groups=mesh['dp'=1,'yax'=2,'xax'=4] {'xax'}, use_global_device_ids=true, to_apply=%region_3.0 | all-reduce | flops 2392064 | bytes 14352384 | tf_op jit(solution)/shard_map/psum | solution.py:75
  210.4 3.7 all-to-all-start
  215.0 7.7 %all-to-all-done = bf16[128,16,128]{2,1,0:T(8,128)(2,1)S(1)} async-done(((bf16[128,16,128]{2,1,0:T(8,128)(2,1)}), bf16[128,16,128]{2,1,0:T(8,128)(2,1)S(1)}, u32[]{:S(2)}, u32[]{:S(2)}) %all-to-all-start) | async-done | bytes 524320 | tf_op jit(solution)/shard_map/all_to_all | solution.py:84
  222.9 23.1 %select_reduce_fusion = (f32[16,32]{1,0:T(8,128)S(1)}, f32[16,32,8192]{2,1,0:T(8,128)}) fusion(pred[16,8192]{1,0:T(8,128)(4,1)S(1)} %iota_compare_fusion, bf16[16,8192,128]{2,1,0:T(8,128)(2,1)} %param.16, bf16[64,32,128]{2,1,0:T(8,128)(2,1)S(1)} %bitcast.58, s32[]{:T(128)S(6)} %select_n.16), kind=kOutput, calls=%fused_computation.2 | convolution fusion | flops 1086324224 | bytes 50595844 | tf_op jit(solution)/shard_map/bhe,bse->bhs/dot_general | solution.py:35
  246.0 8.2 %fusion = f32[16,32]{1,0:T(8,128)S(1)} fusion(f32[16,32,8192]{2,1,0:T(8,128)} %get-tuple-element.23, f32[16,32]{1,0:T(8,128)S(1)} %multiply_maximum_fusion, pred[16,8192]{1,0:T(8,128)(4,1)S(1)} %iota_compare_fusion), kind=kLoop, calls=%fused_computation.3 | loop fusion | flops 16776704 | bytes 16912384 | tf_op jit(solution)/shard_map/reduce_sum | solution.py:41
  254.2 18.9 %fusion.14 = bf16[16,32,128]{2,1,0:T(8,128)(2,1)S(1)} fusion(bf16[16,8192,128]{2,1,0:T(8,128)(2,1)} %param.17, f32[16,32,8192]{2,1,0:T(8,128)} %get-tuple-element.23, f32[16,32]{1,0:T(8,128)S(1)} %get-tuple-element.17, f32[16,32]{1,0:T(8,128)S(1)} %multiply_maximum_fusion, pred[16,8192]{1,0:T(8,128)(4,1)S(1)} %iota_compare_fusion, ...), kind=kOutput, calls=%fused_computation.24 | convolution fusion | flops 1094909952 | bytes 50608128 | tf_op jit(solution)/shard_map/bhs,bse->bhe/dot_general | solution.py:44
  273.1 9.7 %all_gather.3 = bf16[64,32,128]{2,1,0:T(8,128)(2,1)S(1)} all-gather(bf16[16,32,128]{2,1,0:T(8,128)(2,1)S(1)} %fusion.14), channel_id=1, replica_groups=mesh['dp'=1,'yax'=2,'xax'=4] {'xax'}, dimensions={0}, use_global_device_ids=true | all-gather | bytes 655360 | tf_op jit(solution)/shard_map/all_gather | solution.py:90
  283.7 3.5 all-to-all-start.1
  287.3 9.9 %fusion.8 = f32[128,1024]{1,0:T(8,128)S(1)} fusion(bf16[8192,1024]{1,0:T(8,128)(2,1)} %param.25, bf16[128,18688]{1,0:T(8,128)(2,1)} %all-reduce.4), kind=kOutput, calls=%fused_computation.17 | convolution fusion | flops 2155872256 | bytes 21495808 | tf_op jit(solution)/shard_map/dot_general | solution.py:95
  297.5 3.7 convolution_add_fusion
  301.3 23.8 %all-reduce.3.cloned.1.call-done = f32[128,1024]{1,0:T(8,128)} async-done(((f32[128,1024]{1,0:T(8,128)}), f32[128,1024]{1,0:T(8,128)}) %all-reduce.3.cloned.1.call-update) | async-done | bytes 524304 | tf_op jit(solution)/shard_map/psum | solution.py:96
  326.3 6.5 %psum.38 = f32[2,128]{1,0:T(2,128)S(1)} all-reduce(f32[2,128]{1,0:T(2,128)S(1)} %pad_maximum_fusion.2), channel_id=1, replica_groups=mesh['dp'=1,'yax'=2,'xax'=4] {'xax'}, use_global_device_ids=true, to_apply=%region_9.10 | all-reduce | flops 256 | bytes 2048 | tf_op jit(solution)/shard_map/psum | solution.py:27
  332.8 24.6 %fusion.21 = f32[128,25216]{0,1:T(8,128)} fusion(bf16[25216,1024]{1,0:T(8,128)(2,1)} %param.27, f32[1024]{0:T(1024)S(1)} %copy-done.4, f32[128]{0:T(128)S(1)} %fusion.37, f32[128]{0:T(128)S(1)} %multiply_bitcast_fusion, f32[128,1024]{1,0:T(8,128)} %all-reduce.3.cloned.1.call-done, bf16[128,1024]{1,0:T(8,128)(2,1)S(1)} %copy-done.2), kind=kOutput, calls=%fused_computation.44 | convolution fusion | flops 6611009536 | bytes 65344512 | tf_op jit(solution)/shard_map/bd,vd->bv/dot_general | solution.py:98
  357.5 92.3 %reduce-scatter.2.cloned.1.call-done = f32[128,6304]{0,1:T(8,128)} async-done(((f32[128,25216]{0,1:T(8,128)}), f32[128,6304]{0,1:T(8,128)}) %reduce-scatter.2.cloned.1.call-update) | async-done | bytes 3227664 | tf_op jit(solution)/shard_map/reduce_scatter | solution.py:99
  449.7 2.8 reduce_max.19
  452.5 22.2 %pmax.7 = f32[128]{0:T(128)S(1)} all-reduce(f32[128]{0:T(128)S(1)} %reduce_max.19), channel_id=1, replica_groups=mesh['dp'=1,'yax'=2,'xax'=4] {'yax','xax'}, use_global_device_ids=true, to_apply=%region_12.13 | all-reduce | flops 128 | bytes 1024 | tf_op jit(solution)/shard_map/pmax | solution.py:100
  474.7 2.8 exponential_reduce_fusion
  477.5 24.0 %psum.39 = f32[128]{0:T(128)S(1)} all-reduce(f32[128]{0:T(128)S(1)} %exponential_reduce_fusion), channel_id=1, replica_groups=mesh['dp'=1,'yax'=2,'xax'=4] {'yax','xax'}, use_global_device_ids=true, to_apply=%region_14.15 | all-reduce | flops 128 | bytes 1024 | tf_op jit(solution)/shard_map/psum | solution.py:101
  501.5 3.8 broadcast_subtract_fusion
  (58 shorter events, 11.0 us)
Async XLA Ops:
  7.2 14.2 %copy-start = (bf16[1024,128]{1,0:T(8,128)(2,1)S(1)}, bf16[1024,128]{1,0:T(8,128)(2,1)}, u32[]{:S(2)}) copy-start(bf16[1024,128]{1,0:T(8,128)(2,1)} %param.20) | copy-start | bytes 786436
  17.1 18.6 %slice-start = ((s8[16777216]{0:T(1024)(128)(4,1)}), s8[4194304]{0:T(1024)(128)(4,1)S(1)}, s32[]{:S(2)}) async-start(s8[16777216]{0:T(1024)(128)(4,1)} %bitcast.51), calls=%async_computation.5 | async-start | bytes 8388608
  25.2 10.5 %slice-start.1 = ((s8[16777216]{0:T(1024)(128)(4,1)}), s8[4194304]{0:T(1024)(128)(4,1)S(1)}, s32[]{:S(2)}) async-start(s8[16777216]{0:T(1024)(128)(4,1)} %bitcast.51), calls=%async_computation.6 | async-start | bytes 8388608
  25.2 10.5 %slice-start.2 = ((s8[16777216]{0:T(1024)(128)(4,1)}), s8[4194304]{0:T(1024)(128)(4,1)S(1)}, s32[]{:S(2)}) async-start(s8[16777216]{0:T(1024)(128)(4,1)} %bitcast.51), calls=%async_computation.7 | async-start | bytes 8388608
  25.2 10.5 %slice-start.3 = ((s8[16777216]{0:T(1024)(128)(4,1)}), s8[4194304]{0:T(1024)(128)(4,1)S(1)}, s32[]{:S(2)}) async-start(s8[16777216]{0:T(1024)(128)(4,1)} %bitcast.51), calls=%async_computation.8 | async-start | bytes 8388608
  25.2 10.5 %copy-start.2 = (bf16[128,1024]{1,0:T(8,128)(2,1)S(1)}, bf16[128,1024]{1,0:T(8,128)(2,1)}, u32[]{:S(2)}) copy-start(bf16[128,1024]{1,0:T(8,128)(2,1)} %param.14) | copy-start | bytes 786436
  25.2 10.5 %copy-start.3 = (f32[1024]{0:T(1024)S(1)}, f32[1024]{0:T(1024)}, u32[]{:S(2)}) copy-start(f32[1024]{0:T(1024)} %param.18) | copy-start | bytes 12292
  40.2 168.0 %copy-start.7 = (s32[128]{0:T(128)S(1)}, s32[128]{0:T(128)}, u32[]{:S(2)}) copy-start(s32[128]{0:T(128)} %param.15) | copy-start | bytes 1540
  210.4 12.3 %all-to-all-start = ((bf16[128,16,128]{2,1,0:T(8,128)(2,1)}), bf16[128,16,128]{2,1,0:T(8,128)(2,1)S(1)}, u32[]{:S(2)}, u32[]{:S(2)}) async-start(bf16[128,16,128]{2,1,0:T(8,128)(2,1)} %pad_maximum_fusion), calls=%async_computation | async-start | bytes 1048576 | tf_op jit(solution)/shard_map/all_to_all | solution.py:84
  214.4 31.6 %copy-start.5 = (bf16[16,128]{1,0:T(8,128)(2,1)}, bf16[16,128]{1,0:T(8,128)(2,1)S(1)}, u32[]{:S(2)}) copy-start(bf16[16,128]{1,0:T(8,128)(2,1)S(1)} %fusion.32) | copy-start | bytes 12292
  283.7 13.4 %all-to-all-start.1 = ((bf16[64,32,128]{2,0,1:T(8,128)(2,1)}), bf16[64,32,128]{2,0,1:T(8,128)(2,1)S(1)}, u32[]{:S(2)}, u32[]{:S(2)}) async-start(bf16[64,32,128]{2,0,1:T(8,128)(2,1)} %copy.28), calls=%async_computation.1 | async-start | bytes 1048576 | tf_op jit(solution)/shard_map/all_to_all | solution.py:91
  287.2 45.6 %copy-start.4 = (f32[1024]{0:T(1024)S(1)}, f32[1024]{0:T(1024)}, u32[]{:S(2)}) copy-start(f32[1024]{0:T(1024)} %param.26) | copy-start | bytes 12292
  287.2 37.8 %all-reduce.3.cloned.1.call-start = ((), (), s32[]{:S(2)}) async-start(), calls=%async_computation.3 | async-start | bytes 1048576 | tf_op jit(solution)/shard_map/psum | solution.py:96
  301.2 148.5 %reduce-scatter.2.cloned.1.call-start = ((), (), s32[]{:S(2)}) async-start(), calls=%async_computation.4 | async-start | bytes 16138240 | tf_op jit(solution)/shard_map/reduce_scatter | solution.py:99
  357.4 147.8 %copy-start.1 = (bf16[1024,128]{1,0:T(8,128)(2,1)S(1)}, bf16[1024,128]{1,0:T(8,128)(2,1)}, u32[]{:S(2)}) copy-start(bf16[1024,128]{1,0:T(8,128)(2,1)} %param.20) | copy-start | bytes 786436
  501.4 3.8 copy-start.6
Sparse Core Ops, SparseCore 0:
  301.4 23.6 all-reduce.2
  357.6 92.0 reduce-scatter.1
where the time goes:
time: 513 us; the launch traced here: 512 us
  blocking collectives  237 us (46%)
  waiting for transfers between devices  124 us (24%)
  matrix products  103 us (20%)
  other arithmetic  24.6 us (5%)
  between operations  14.3 us (3%)
  starting transfers between devices  7.24 us (1%)
    psum x1, blocking collectives, local_step(): projected = lax.psum(proj_part, 'xax').astype(jnp.bfloat16)  166 us
    reduce_scatter x1, waiting for transfers between devices, local_step(): lax.psum_scatter(logit_part, 'xax', scatter_dimension=1, tiled=True)  92.3 us
    dot_general x1, matrix products, local_step(): jnp.einsum('bd,vd->bv', final_norm, embedding, preferred_element_type=jnp...  24.6 us
    psum x1, blocking collectives, local_step(): lax.psum(jnp.sum(jnp.exp(logits - row_max[:, None]), axis=1), ('yax', 'xa...  24 us
    psum x1, waiting for transfers between devices, local_step(): residual_out = residual + lax.psum(branch_sum, 'yax')  23.8 us
    dot_general x1, matrix products, attend_local(): jnp.einsum('bhe,bse->bhs', query, k_cache, preferred_element_type=jnp.flo...  23.1 us
    pmax x1, blocking collectives, local_step(): row_max = lax.pmax(jnp.max(logits, axis=1), ('yax', 'xax'))  22.2 us
    dot_general x1, matrix products, attend_local(): jnp.einsum('bhs,bse->bhe', prob_all, v_cache, preferred_element_type=jnp....  18.9 us
  transfers between devices with their start and end apart: 4, of which 3 were waited for; matrix products, arithmetic and copies ran while one was open for 2% of the time, Pallas kernels for 0%

commit v1 on v0

v1 whole, which is shorter than its diff:
```python
import functools

import jax
import jax.numpy as jnp
from jax import lax
from jax.experimental import pallas as pl
from jax.experimental.pallas import tpu as pltpu
from jax.sharding import PartitionSpec as P

EPS = 1e-6
ROPE_BASE = 10000.0
MESH = pl.DeviceIdType.MESH
F32 = jnp.float32
BF16 = jnp.bfloat16
LOW = -3e38


def place():
    y = lax.axis_index("yax")
    xi = lax.axis_index("xax")
    chip = xi // 2
    core = xi % 2
    return y, xi, chip, core, chip * 2 + (1 - core), (1 - chip) * 2 + core


def send(src, dst, send_sem, recv_sem, y, xi):
    return pltpu.make_async_remote_copy(src_ref=src, dst_ref=dst, send_sem=send_sem, recv_sem=recv_sem,
                                        device_id={"yax": y, "xax": xi}, device_id_type=MESH)


def enter(peers):
    barrier = pltpu.get_barrier_semaphore()
    for y, xi in peers:
        pl.semaphore_signal(barrier, inc=1, device_id={"yax": y, "xax": xi}, device_id_type=MESH)
    return lambda: pl.semaphore_wait(barrier, len(peers))


def to_lanes(first, second):
    rows = first.shape[0]
    lane = lax.broadcasted_iota(jnp.int32, (rows, 128), 1)
    tile = jnp.where(lane == 0, first, jnp.where(lane == 1, second, 0.0))
    if rows < 128:
        tile = jnp.concatenate([tile, jnp.zeros((128 - rows, 128), F32)], axis=0)
    return tile.T[:8]


def to_columns(first, second):
    row = lax.broadcasted_iota(jnp.int32, (128, 128), 0)
    tile = jnp.where(row == 0, first, jnp.where(row == 1, second, 0.0)).T
    return tile[:, 0:1], tile[:, 1:2]


def norm_stats(values, stat, y, xi, send_sems, recv_sems, ready, size):
    rows, width = values.shape
    mean_own = jnp.sum(values, axis=1, keepdims=True) / width
    diff = values - mean_own
    stat[xi] = to_lanes(mean_own, jnp.sum(diff * diff, axis=1, keepdims=True))
    ready()
    copies = [send(stat.at[xi], stat.at[xi], send_sems.at[d - 1], recv_sems.at[d - 1], y, (xi + d) % size)
              for d in range(1, size)]
    for copy in copies:
        copy.start()
    for copy in copies:
        copy.wait()
    tiles = [stat[i] for i in range(size)]
    mean_all = sum(t[0:1] for t in tiles) / size
    spread = sum(t[1:2] for t in tiles) + width * sum((t[0:1] - mean_all) * (t[0:1] - mean_all) for t in tiles)
    mean_col, rstd_col = to_columns(mean_all, lax.rsqrt(spread / (width * size) + EPS))
    return mean_col[:rows], rstd_col[:rows]


def qkv_kernel(hid, gain, cos, sin, wq, wk, wv, q_out, k_out, v_out, n_out,
               w_all, part, got_a, sum_b, got_b, total, q_rot, q_full, stat,
               w_sem, stat_s, stat_r, pair_s, pair_r):
    y, xi, chip, core, partner, twin = place()
    qc = wq.shape[1]
    hd = wk.shape[1]
    loads = [pltpu.make_async_copy(wq, w_all.at[:, pl.ds(0, qc)], w_sem.at[0]),
             pltpu.make_async_copy(wk, w_all.at[:, pl.ds(qc, hd)], w_sem.at[1]),
             pltpu.make_async_copy(wv, w_all.at[:, pl.ds(qc + hd, hd)], w_sem.at[2])]
    for load in loads:
        load.start()
    ready = enter([(y, (xi + d) % 4) for d in (1, 2, 3)] + [(1 - y, xi)])
    h = hid[...].astype(F32)
    mean, rstd = norm_stats(h, stat, y, xi, stat_s, stat_r, ready, 4)
    normed = ((h - mean) * rstd * gain[...]).astype(BF16)
    for core_o in range(2):
        for chip_o in range(2):
            for y_o in range(2):
                src = (y_o * 4 + chip_o * 2 + core_o) * 16
                dst = (core_o * 4 + chip_o * 2 + y_o) * 16
                n_out[dst:dst + 16, :] = normed[src:src + 16, :]
    for load in loads:
        load.wait()
    step = 256

    def project(i, carry):
        cols = pl.ds(pl.multiple_of(i * step, step), step)
        prod = jnp.dot(n_out[...], w_all[:, cols], preferred_element_type=F32)
        part[:, :, :, cols] = prod.reshape(2, 2, 32, step)
        return carry

    lax.fori_loop(0, (qc + 2 * hd) // step, project, 0)
    hop_a = send(part.at[1 - core], got_a, pair_s.at[0], pair_r.at[0], y, partner)
    hop_a.start()
    hop_a.wait_recv()
    sum_b[...] = part[core, 1 - chip] + got_a[1 - chip]
    hop_b = send(sum_b, got_b, pair_s.at[1], pair_r.at[1], y, twin)
    hop_b.start()
    own = part[core, chip] + got_a[chip]
    hop_b.wait_recv()
    total[...] = (own + got_b[...]).astype(BF16).astype(F32).reshape(2, 16, qc + 2 * hd)
    for y_o in range(2):
        block = y_o * 4 + chip * 2 + core
        cos_r, sin_r = cos[block], sin[block]
        for head in range(qc // hd):
            val = total[y_o, :, head * hd:(head + 1) * hd]
            q_rot[y_o, :, head * hd:(head + 1) * hd] = (val * cos_r + pltpu.roll(val, hd // 2, 1) * sin_r).astype(BF16)
    hop_c = send(q_rot.at[1 - y], q_full.at[y], pair_s.at[2], pair_r.at[2], 1 - y, xi)
    hop_c.start()
    mine = y * 4 + chip * 2 + core
    key = total[y, :, qc:qc + hd]
    k_out[...] = (key * cos[mine] + pltpu.roll(key, hd // 2, 1) * sin[mine]).astype(BF16)
    v_out[...] = total[y, :, qc + hd:qc + 2 * hd].astype(BF16)
    q_out[y] = q_rot[y]
    hop_c.wait_recv()
    q_out[1 - y] = q_full[1 - y]
    hop_a.wait_send()
    hop_b.wait_send()
    hop_c.wait_send()


def qkv_call(hid, gain, cos, sin, wq, wk, wv):
    rows, width = hid.shape
    qc, hd = wq.shape[1], wk.shape[1]
    cols = qc + 2 * hd
    vmem = pl.BlockSpec(memory_space=pltpu.VMEM)
    hbm = pl.BlockSpec(memory_space=pl.ANY)
    return pl.pallas_call(
        qkv_kernel, name="qkv",
        out_shape=[jax.ShapeDtypeStruct((2, 16, qc), BF16), jax.ShapeDtypeStruct((16, hd), BF16),
                   jax.ShapeDtypeStruct((16, hd), BF16), jax.ShapeDtypeStruct((rows, width), BF16)],
        in_specs=[vmem] * 4 + [hbm] * 3, out_specs=[vmem] * 4,
        scratch_shapes=[
            pltpu.VMEM((width, cols), BF16), pltpu.VMEM((2, 2, 32, cols), F32), pltpu.VMEM((2, 32, cols), F32),
            pltpu.VMEM((32, cols), F32), pltpu.VMEM((32, cols), F32), pltpu.VMEM((2, 16, cols), F32),
            pltpu.VMEM((2, 16, qc), BF16), pltpu.VMEM((2, 16, qc), BF16), pltpu.VMEM((4, 8, 128), F32),
            pltpu.SemaphoreType.DMA((3,)), pltpu.SemaphoreType.DMA((3,)), pltpu.SemaphoreType.DMA((3,)),
            pltpu.SemaphoreType.DMA((3,)), pltpu.SemaphoreType.DMA((3,))],
        compiler_params=pltpu.CompilerParams(collective_id=0, has_side_effects=True, vmem_limit_bytes=60 * 2**20),
    )(hid, gain, cos, sin, wq, wk, wv)


CHUNK = 1024
SLOTS = 4


def attend_kernel(lens, q_ref, kn_ref, vn_ref, k_hbm, v_hbm, o_ref, k_buf, v_buf, scores, k_sem, v_sem):
    seqs = q_ref.shape[0]
    scale = q_ref.shape[2] ** -0.5

    def chunks(b):
        return (lens[b] + CHUNK - 1) // CHUNK

    def fetch(b):
        slot = b % SLOTS

        def one(i, carry):
            rows = pl.ds(pl.multiple_of(i * CHUNK, CHUNK), CHUNK)
            pltpu.make_async_copy(k_hbm.at[b, rows], k_buf.at[slot, rows], k_sem.at[slot, i]).start()
            pltpu.make_async_copy(v_hbm.at[b, rows], v_buf.at[slot, rows], v_sem.at[slot, i]).start()
            return carry

        lax.fori_loop(0, chunks(b), one, 0)

    for b in range(SLOTS - 1):
        fetch(b)

    def sequence(b, carry):
        slot = b % SLOTS

        @pl.when(b + SLOTS - 1 < seqs)
        def _():
            fetch(b + SLOTS - 1)

        q = q_ref[b]
        length = lens[b]
        s_new = jnp.sum(q.astype(F32) * kn_ref[b].astype(F32), axis=1, keepdims=True) * scale

        def score(i, top):
            rows = pl.ds(pl.multiple_of(i * CHUNK, CHUNK), CHUNK)
            pltpu.make_async_copy(k_hbm.at[b, rows], k_buf.at[slot, rows], k_sem.at[slot, i]).wait()
            s = lax.dot_general(q, k_buf[slot, rows], (((1,), (1,)), ((), ())), preferred_element_type=F32) * scale
            pos = lax.broadcasted_iota(jnp.int32, s.shape, 1) + i * CHUNK
            s = jnp.where(pos < length, s, -jnp.inf)
            scores[i] = s
            return jnp.maximum(top, jnp.max(s, axis=1, keepdims=True))

        count = chunks(b)
        top = lax.fori_loop(0, count, score, s_new)

        def weigh(i, acc):
            e = jnp.exp(scores[i] - top)
            scores[i] = e
            return acc + jnp.sum(e, axis=1, keepdims=True)

        e_new = jnp.exp(s_new - top)
        inv = 1.0 / lax.fori_loop(0, count, weigh, e_new)

        def mix(i, acc):
            rows = pl.ds(pl.multiple_of(i * CHUNK, CHUNK), CHUNK)
            pltpu.make_async_copy(v_hbm.at[b, rows], v_buf.at[slot, rows], v_sem.at[slot, i]).wait()
            p = (scores[i] * inv).astype(BF16)
            return acc + jnp.dot(p, v_buf[slot, rows], preferred_element_type=F32)

        o_new = (e_new * inv).astype(BF16).astype(F32) * vn_ref[b].astype(F32)
        o_ref[b] = lax.fori_loop(0, count, mix, o_new).astype(BF16)
        return carry

    lax.fori_loop(0, seqs, sequence, 0)


def attend_call(lens, q, k_new, v_new, k_cache, v_cache):
    seqs, heads, hd = q.shape
    length = k_cache.shape[1]
    vmem = pl.BlockSpec(memory_space=pltpu.VMEM)
    hbm = pl.BlockSpec(memory_space=pl.ANY)
    return pl.pallas_call(
        attend_kernel, name="attend",
        out_shape=jax.ShapeDtypeStruct((seqs, heads, hd), BF16),
        in_specs=[pl.BlockSpec(memory_space=pltpu.SMEM)] + [vmem] * 3 + [hbm] * 2, out_specs=vmem,
        scratch_shapes=[
            pltpu.VMEM((SLOTS, length, hd), BF16), pltpu.VMEM((SLOTS, length, hd), BF16),
            pltpu.VMEM((length // CHUNK, heads, CHUNK), F32),
            pltpu.SemaphoreType.DMA((SLOTS, length // CHUNK)), pltpu.SemaphoreType.DMA((SLOTS, length // CHUNK))],
        compiler_params=pltpu.CompilerParams(vmem_limit_bytes=60 * 2**20),
    )(lens, q, k_new.reshape(seqs, 1, hd), v_new.reshape(seqs, 1, hd), k_cache, v_cache)


FC = 512
RING = 4


def mlp_kernel(normed, o_in, hid, gain, wg, wu, wo, wd, f_out,
               w_ring, wd_all, wo_all, part, got_a, sum_b, got_b, act, o_all, acc, y_got, f_all, stat,
               w_sem, wd_sem, wo_sem, a_s, a_r, b_s, b_r, m_s, m_r, p_s, p_r, o_s, o_r, stat_s, stat_r):
    y, xi, chip, core, partner, twin = place()
    steps = part.shape[0]
    ready = enter([(y, (xi + d) % 4) for d in (1, 2, 3)] + [(1 - y, xi)])

    def w_loads(j):
        cols = pl.ds(pl.multiple_of(j * FC, FC), FC)
        slot = j % RING
        return (pltpu.make_async_copy(wg.at[:, cols], w_ring.at[slot, 0], w_sem.at[slot, 0]),
                pltpu.make_async_copy(wu.at[:, cols], w_ring.at[slot, 1], w_sem.at[slot, 1]))

    def wd_load(j):
        return pltpu.make_async_copy(wd.at[pl.ds(pl.multiple_of(j * FC, FC), FC)], wd_all.at[j], wd_sem.at[j])

    def hop_a(j):
        return send(part.at[j, 1 - core], got_a.at[j], a_s.at[j], a_r.at[j], y, partner)

    def hop_b(j):
        return send(sum_b.at[j], got_b.at[j], b_s.at[j], b_r.at[j], y, twin)

    def hop_m(j):
        return send(act.at[j, core, chip], act.at[j, core, chip], m_s.at[j], m_r.at[j], y, twin)

    def hop_p(j):
        return send(act.at[j, core], act.at[j, core], p_s.at[j], p_r.at[j], y, partner)

    for j in range(RING - 1):
        for load in w_loads(j):
            load.start()
    hop_o0 = send(o_in.at[1 - y], o_all.at[core, chip, y], o_s.at[0], o_r.at[0], 1 - y, xi)
    hop_o1 = send(o_all.at[core, chip], o_all.at[core, chip], o_s.at[1], o_r.at[1], y, twin)
    hop_o2 = send(o_all.at[core], o_all.at[core], o_s.at[2], o_r.at[2], y, partner)
    o_all[core, chip, y] = o_in[y]
    ready()
    hop_o0.start()

    def add_pair(j):
        hop_a(j).wait_recv()
        sum_b[j] = part[j, core, 1 - chip] + got_a[j, 1 - chip]
        hop_b(j).start()

    def project(j, carry):
        @pl.when(j + RING - 1 < steps)
        def _():
            for load in w_loads(j + RING - 1):
                load.start()

        @pl.when(j + RING - 1 >= steps)
        def _():
            wd_load(j + RING - 1 - steps).start()

        slot = j % RING
        for i, load in enumerate(w_loads(j)):
            load.wait()
            prod = jnp.dot(normed[...], w_ring[slot, i], preferred_element_type=F32)
            part[j, :, :, :, i * FC:(i + 1) * FC] = prod.reshape(2, 2, 32, FC)
        hop_a(j).start()

        @pl.when(j >= 1)
        def _():
            add_pair(j - 1)
        return carry

    lax.fori_loop(0, steps, project, 0)
    for j in range(RING - 1, steps):
        wd_load(j).start()
    load_o = pltpu.make_async_copy(wo, wo_all, wo_sem)
    load_o.start()
    add_pair(steps - 1)
    hop_o0.wait_recv()
    hop_o1.start()
    acc[...] = jnp.zeros_like(acc)

    def activate(j):
        hop_b(j).wait_recv()
        both = part[j, core, chip] + got_a[j, chip] + got_b[j]
        gate = both[:, :FC].astype(BF16).astype(F32)
        up_val = both[:, FC:].astype(BF16).astype(F32)
        act[j, core, chip] = (jax.nn.silu(gate) * up_val).astype(BF16)
        hop_m(j).start()

    def pass_on(j):
        hop_m(j).wait_recv()
        hop_p(j).start()

    def contract(j):
        hop_p(j).wait_recv()
        wd_load(j).wait()
        acc[...] += jnp.dot(act[j].reshape(128, FC), wd_all[j], preferred_element_type=F32).reshape(acc.shape)

    def reduce(j, carry):
        @pl.when(j < steps)
        def _():
            activate(j)

        @pl.when((j >= 1) & (j < steps + 1))
        def _():
            pass_on(j - 1)

        @pl.when(j == 1)
        def _():
            hop_o1.wait_recv()
            hop_o2.start()

        @pl.when(j == 2)
        def _():
            hop_o2.wait_recv()
            load_o.wait()
            part_o = jnp.dot(o_all[...].reshape(128, o_all.shape[-1]), wo_all[...], preferred_element_type=F32)
            acc[...] += part_o.reshape(acc.shape)

        @pl.when(j >= 2)
        def _():
            contract(j - 2)
        return carry

    lax.fori_loop(0, steps + 2, reduce, 0)

    width = acc.shape[-1]
    hop_y = send(acc.at[:, 1 - y], y_got, o_s.at[3], o_r.at[3], 1 - y, xi)
    hop_y.start()
    hop_y.wait_recv()
    res = [hid[y * 4 + (i % 2) * 2 + i // 2].astype(F32) for i in range(4)]
    branch = acc[:, y] + y_got[...]
    r = jnp.concatenate(res, axis=0) + branch.reshape(64, width)
    mean, rstd = norm_stats(r, stat, y, xi, stat_s, stat_r, lambda: None, 4)
    f = ((r - mean) * rstd * gain[...]).astype(BF16)
    for i in range(4):
        f_all[y, (i % 2) * 2 + i // 2] = f[i * 16:(i + 1) * 16]
    hop_f = send(f_all.at[y], f_all.at[y], o_s.at[4], o_r.at[4], 1 - y, xi)
    hop_f.start()
    f_out[y] = f_all[y]
    hop_f.wait_recv()
    f_out[1 - y] = f_all[1 - y]

    def drain(j, carry):
        hop_a(j).wait_send()
        hop_b(j).wait_send()
        hop_m(j).wait_send()
        hop_p(j).wait_send()
        return carry

    lax.fori_loop(0, steps, drain, 0)
    for hop in (hop_o0, hop_o1, hop_o2, hop_y, hop_f):
        hop.wait_send()


def mlp_call(normed, o_in, hid, gain, wg, wu, wo, wd):
    width = normed.shape[1]
    steps = wg.shape[1] // FC
    oc = wo.shape[0]
    vmem = pl.BlockSpec(memory_space=pltpu.VMEM)
    hbm = pl.BlockSpec(memory_space=pl.ANY)
    dma = pltpu.SemaphoreType.DMA
    return pl.pallas_call(
        mlp_kernel, name="mlp",
        out_shape=jax.ShapeDtypeStruct((2, 4, 16, width), BF16),
        in_specs=[vmem] * 4 + [hbm] * 4, out_specs=vmem,
        scratch_shapes=[
            pltpu.VMEM((RING, 2, width, FC), BF16), pltpu.VMEM((steps, FC, width), BF16), pltpu.VMEM((oc, width), BF16),
            pltpu.VMEM((steps, 2, 2, 32, 2 * FC), F32), pltpu.VMEM((steps, 2, 32, 2 * FC), F32),
            pltpu.VMEM((steps, 32, 2 * FC), F32), pltpu.VMEM((steps, 32, 2 * FC), F32),
            pltpu.VMEM((steps, 2, 2, 32, FC), BF16), pltpu.VMEM((2, 2, 2, 16, oc), BF16),
            pltpu.VMEM((4, 2, 16, width), F32), pltpu.VMEM((4, 16, width), F32), pltpu.VMEM((2, 4, 16, width), BF16),
            pltpu.VMEM((4, 8, 128), F32),
            dma((RING, 2)), dma((steps,)), dma, dma((steps,)), dma((steps,)), dma((steps,)), dma((steps,)),
            dma((steps,)), dma((steps,)), dma((steps,)), dma((steps,)), dma((5,)), dma((5,)), dma((3,)), dma((3,))],
        compiler_params=pltpu.CompilerParams(collective_id=1, has_side_effects=True, vmem_limit_bytes=60 * 2**20),
    )(normed, o_in, hid, gain, wg, wu, wo, wd)


VC = 512
ERING = 8


def head_kernel(share, f_ref, emb, z_out, lse_out,
                e_ring, e_tail, buf_a, buf_b, buf_c, buf_d, got_a, got_b, got_c,
                t_a, t_b, t_c, t_d, tg_a, tg_b, tg_c, top, total, stat,
                e_sem, tail_sem, a_s, a_r, b_s, b_r, c_s, c_r, t_s, t_r, stat_s, stat_r):
    y, xi, chip, core, partner, twin = place()
    full = share // VC
    rest = share - full * VC
    tail = full * VC
    ready = enter([(y, (xi + d) % 4) for d in (1, 2, 3)] + [(1 - y, (xi + d) % 4) for d in range(4)])
    far = (1 - chip) * 2
    near = chip * 2

    def share_of(i):
        side = i // 2
        mine = i % 2
        base = far + side * (near - far)
        return base + (1 - core) + mine * (2 * core - 1)

    def e_load(t):
        k = (t // 2) % full
        i = (t // (2 * full)) * 2 + t % 2
        rows = pl.ds(pl.multiple_of(share_of(i) * share + k * VC, 32), VC)
        return pltpu.make_async_copy(emb.at[rows], e_ring.at[t % ERING], e_sem.at[t % ERING])

    def tail_load(i):
        rows = pl.ds(pl.multiple_of(share_of(i) * share + tail, 32), rest)
        return pltpu.make_async_copy(emb.at[rows], e_tail.at[i], tail_sem.at[i])

    for i in range(4):
        tail_load(i).start()
    for t in range(ERING - 1):
        e_load(t).start()

    def hop_a(k):
        return send(buf_a.at[k], got_a.at[k], a_s.at[k], a_r.at[k], y, partner)

    def hop_b(k):
        return send(buf_b.at[k], got_b.at[k], b_s.at[k], b_r.at[k], y, twin)

    def hop_c(k):
        return send(buf_c.at[k], got_c.at[k], c_s.at[k], c_r.at[k], y, partner)

    hop_ta = send(t_a, tg_a, t_s.at[0], t_r.at[0], y, partner)
    hop_tb = send(t_b, tg_b, t_s.at[1], t_r.at[1], y, twin)
    hop_tc = send(t_c, tg_c, t_s.at[2], t_r.at[2], y, partner)

    def product(e):
        return lax.dot_general(f_ref[...], e, (((1,), (1,)), ((), ())), preferred_element_type=F32)

    for t_ref in (t_a, t_b, t_c, t_d):
        t_ref[...] = jnp.zeros_like(t_ref)

    def tail_product(i, t_ref):
        tail_load(i).wait()
        t_ref[:, :rest] = product(e_tail[i])

    def chunk_product(t, buf, k):
        @pl.when(t + ERING - 1 < 4 * full)
        def _():
            e_load(t + ERING - 1).start()

        e_load(t).wait()
        buf[k] = product(e_ring[t % ERING])

    tail_product(0, t_a)
    ready()
    hop_ta.start()
    tail_product(1, t_b)
    hop_ta.wait_recv()
    t_b[...] += tg_a[...]
    hop_tb.start()

    def add_pair(k):
        hop_a(k).wait_recv()
        buf_b[k] += got_a[k]
        hop_b(k).start()

    def outward(k, carry):
        chunk_product(2 * k, buf_a, k)
        hop_a(k).start()
        chunk_product(2 * k + 1, buf_b, k)

        @pl.when(k >= 1)
        def _():
            add_pair(k - 1)
        return carry

    lax.fori_loop(0, full, outward, 0)
    add_pair(full - 1)
    tail_product(2, t_c)
    hop_tc.start()
    tail_product(3, t_d)

    def inward(k, carry):
        chunk_product(2 * full + 2 * k, buf_c, k)
        hop_c(k).start()
        chunk_product(2 * full + 2 * k + 1, buf_d, k)
        return carry

    lax.fori_loop(0, full, inward, 0)

    top[...] = jnp.full_like(top, LOW)
    total[...] = jnp.zeros_like(total)

    def fold(z):
        groups = [z[:, i:i + 128] for i in range(0, z.shape[1], 128)]
        high = functools.reduce(jnp.maximum, groups, top[...])
        total[...] = total[...] * jnp.exp(top[...] - high) + sum(jnp.exp(g - high) for g in groups)
        top[...] = high

    hop_tc.wait_recv()
    hop_tb.wait_recv()
    z_tail = t_d[...] + tg_c[...] + tg_b[...]
    z_out[:, tail:] = z_tail[:, :rest]
    lane = lax.broadcasted_iota(jnp.int32, z_tail.shape, 1)
    fold(jnp.where(lane < rest, z_tail, LOW))

    def finish(k, carry):
        hop_c(k).wait_recv()
        hop_b(k).wait_recv()
        z = buf_d[k] + got_c[k] + got_b[k]
        z_out[:, pl.ds(pl.multiple_of(k * VC, VC), VC)] = z
        fold(z)
        return carry

    lax.fori_loop(0, full, finish, 0)
    high = jnp.max(top[...], axis=1, keepdims=True)
    mass = jnp.sum(total[...] * jnp.exp(top[...] - high), axis=1, keepdims=True)
    me = y * 4 + xi
    stat[me] = to_lanes(high, mass)
    copies = []
    for dy in range(2):
        for d in range(4):
            if dy or d:
                i = dy * 4 + d - 1
                copies.append(send(stat.at[me], stat.at[me], stat_s.at[i], stat_r.at[i],
                                   y + dy * (1 - 2 * y), (xi + d) % 4))
    for copy in copies:
        copy.start()
    for copy in copies:
        copy.wait()
    highs = [stat[i][0:1] for i in range(8)]
    best = functools.reduce(jnp.maximum, highs)
    mass_all = sum(stat[i][1:2] * jnp.exp(highs[i] - best) for i in range(8))
    lse_out[...] = best + jnp.log(mass_all)

    def drain(k, carry):
        hop_a(k).wait_send()
        hop_b(k).wait_send()
        hop_c(k).wait_send()
        return carry

    lax.fori_loop(0, full, drain, 0)
    for hop in (hop_ta, hop_tb, hop_tc):
        hop.wait_send()


def head_call(f, emb):
    rows, width = f.shape
    share = emb.shape[0] // 4
    full = share // VC
    rest = share - full * VC
    vmem = pl.BlockSpec(memory_space=pltpu.VMEM)
    hbm = pl.BlockSpec(memory_space=pl.ANY)
    dma = pltpu.SemaphoreType.DMA
    tail_w = -(-rest // 128) * 128
    return pl.pallas_call(
        functools.partial(head_kernel, share), name="head",
        out_shape=[jax.ShapeDtypeStruct((rows, share), F32), jax.ShapeDtypeStruct((1, rows), F32)],
        in_specs=[vmem, hbm], out_specs=[vmem, vmem],
        scratch_shapes=[pltpu.VMEM((ERING, VC, width), BF16), pltpu.VMEM((4, rest, width), BF16)]
        + [pltpu.VMEM((full, rows, VC), F32)] * 7 + [pltpu.VMEM((rows, tail_w), F32)] * 7
        + [pltpu.VMEM((rows, 128), F32)] * 2 + [pltpu.VMEM((8, 8, 128), F32)]
        + [dma((ERING,)), dma((4,))] + [dma((full,))] * 6 + [dma((3,))] * 2 + [dma((7,))] * 2,
        compiler_params=pltpu.CompilerParams(collective_id=2, has_side_effects=True, vmem_limit_bytes=60 * 2**20),
    )(f, emb)


def solution(mesh):
    row_spec = P(("dp", "yax", "xax"))

    def local_step(hidden, cache_len, k_cache, v_cache, g_attn, w_query, w_key, w_value,
                   w_gate, w_up, w_out, w_down, g_final, embedding):
        rows, width = hidden.shape
        own_rows, _, head_dim = k_cache.shape
        half = head_dim // 2
        own_start = (lax.axis_index("yax") * 4 + lax.axis_index("xax")) * own_rows
        inv_freq = ROPE_BASE ** (-(jnp.arange(half, dtype=F32) * 2.0) / head_dim)
        angles = cache_len.astype(F32)[:, None] * inv_freq[None, :]
        cos_a, sin_a = jnp.cos(angles), jnp.sin(angles)
        cos_t = jnp.concatenate([cos_a, cos_a], axis=1).reshape(8, own_rows, head_dim)
        sin_t = jnp.concatenate([-sin_a, sin_a], axis=1).reshape(8, own_rows, head_dim)

        q, key_own, value_own, normed = qkv_call(hidden, g_attn[None], cos_t, sin_t, w_query, w_key, w_value)
        half_heads = w_query.shape[1] // head_dim
        q = q.reshape(2, own_rows, half_heads, head_dim).transpose(1, 0, 2, 3).reshape(own_rows, 2 * half_heads, head_dim)
        len_own = lax.dynamic_slice_in_dim(cache_len, own_start, own_rows, axis=0)
        attn = attend_call(len_own, q, key_own, value_own, k_cache, v_cache)
        attn = attn.reshape(own_rows, 2, half_heads * head_dim).transpose(1, 0, 2)
        f = mlp_call(normed, attn, hidden.reshape(8, own_rows, width), g_final[None], w_gate, w_up, w_out, w_down)
        logits, log_norm = head_call(f.reshape(rows, width), embedding)
        log_norm = log_norm[0]
        return key_own, value_own, logits - log_norm[:, None], log_norm

    in_specs = (P("dp", "xax"), P("dp"), row_spec, row_spec, P("xax"), P("xax", "yax"),
                P("xax", None), P("xax", None), P("xax", "yax"), P("xax", "yax"),
                P("yax", "xax"), P("yax", "xax"), P("xax"), P("yax", "xax"))
    out_specs = (row_spec, row_spec, P("dp", ("yax", "xax")), P("dp"))
    return jax.shard_map(local_step, mesh=mesh, in_specs=in_specs, out_specs=out_specs, check_vma=False)
```

time: 513 us -> 273 us (0.53)
  Pallas kernels: 0 us -> 253 us
  blocking collectives: 237 us -> 0 us
  waiting for transfers between devices: 124 us -> 0 us
  matrix products: 103 us -> 0 us
  other arithmetic: 24.6 us -> 3.94 us
  between operations: 14.3 us -> 0.72 us
  local copies, waits for them, and re-layouts: 1.71 us -> 11.7 us
  starting transfers between devices: 7.24 us -> 0 us
    pallas_call x0 -> x4, Pallas kernels: none -> 253 us  [the longest x1 102 us: mlp_call(): pl.pallas_call(mlp_kernel, name='mlp', out_shape=jax.ShapeDtypeStruct((2,...]
    psum x4 -> x0, blocking collectives: 205 us -> none  [the longest x1 166 us: local_step(): projected = lax.psum(proj_part, 'xax').astype(jnp.bfloat16)]
    dot_general x11 -> x0, matrix products: 103 us -> none  [the longest x1 24.6 us: local_step(): jnp.einsum('bd,vd->bv', final_norm, embedding, preferred_element_type=jnp...]
    reduce_scatter x1 -> x0, waiting for transfers between devices: 92.3 us -> none  [local_step(): lax.psum_scatter(logit_part, 'xax', scatter_dimension=1, tiled=True)]
    psum x1 -> x0, waiting for transfers between devices: 23.8 us -> none  [local_step(): residual_out = residual + lax.psum(branch_sum, 'yax')]
    pmax x1 -> x0, blocking collectives: 22.2 us -> none  [local_step(): row_max = lax.pmax(jnp.max(logits, axis=1), ('yax', 'xax'))]
    reduce_sum x4 -> x0, other arithmetic: 13.3 us -> none  [the longest x1 8.18 us: attend_local(): denominator = jnp.sum(weights, axis=-1) + weight_new]
    all_gather x1 -> x0, blocking collectives: 9.66 us -> none  [local_step(): attn_grp = lax.all_gather(attn_own, 'xax', axis=0, tiled=True)]
  transfers between devices with their start and end apart: 4 -> 0, of which waited for: 3 -> 0; matrix products, arithmetic and copies ran while one was open for 2% -> 0% of each run, Pallas kernels for 0% -> 0%
where the time goes in v1:
time: 273 us; the launch traced here: 269 us
  Pallas kernels  253 us (93%)
  local copies, waits for them, and re-layouts  11.7 us (4%)
  other arithmetic  3.94 us (1%)
    pallas_call x1, Pallas kernels, mlp_call(): pl.pallas_call(mlp_kernel, name='mlp', out_shape=jax.ShapeDtypeStruct((2,...  102 us
    pallas_call x1, Pallas kernels, head_call(): pl.pallas_call(functools.partial(head_kernel, share), name='head', out_sh...  81.8 us
    pallas_call x1, Pallas kernels, attend_call(): pl.pallas_call(attend_kernel, name='attend', out_shape=jax.ShapeDtypeStru...  45.4 us
    pallas_call x1, Pallas kernels, qkv_call(): pl.pallas_call(qkv_kernel, name='qkv', out_shape=[jax.ShapeDtypeStruct((2...  24.3 us
    unnamed x11, local copies, waits for them, and re-layouts  5.54 us

profile of v1, /device:TPU:0, one launch (start us, length us, event | category | flops | bytes accessed | tf_op | source)
XLA Modules:
  0.0 269.5 jit_solution(15786299447996724346)
XLA Ops:
  0.6 1.2 dynamic_slice.3.lens
  1.9 0.7 convert_element_type.3
  2.5 0.1 mul.35
  2.6 0.3 fusion
  2.9 0.8 pad_maximum_fusion
  3.7 24.3 %qkv.1 = (bf16[2,16,2048]{2,1,0:T(8,128)(2,1)}, bf16[16,128]{1,0:T(8,128)(2,1)}, bf16[16,128]{1,0:T(8,128)(2,1)}, bf16[128,1024]{1,0:T(8,128)(2,1)}) custom-call(bf16[128,1024]{1,0:T(8,128)(2,1)} %hid.1, f32[1,1024]{1,0:T(1,128)} %bitcast.26, f32[8,16,128]{2,1,0:T(8,128)} %get-tuple-element.27.cos, f32[8,16,128]{2,1,0:T(8,128)} %get-tuple-element.28.sin, ...), custom_call_target="tpu_custom_call" | custom-call | tf_op jit(solution)/shard_map/qkv/pallas_call | solution.py:139
  28.0 0.9 copy.25
  29.0 0.7 copy.20
  29.6 1.3 copy.22.vn_ref
  30.9 1.3 copy.21.kn_ref
  32.2 45.4 %attend.1 = bf16[16,32,128]{2,1,0:T(8,128)(2,1)} custom-call(s32[16]{0:T(128)} %dynamic_slice.3.lens, bf16[16,32,128]{2,1,0:T(8,128)(2,1)} %bitcast.19, bf16[16,1,128]{2,1,0:T(2,128)(2,1)} %copy.21.kn_ref, bf16[16,1,128]{2,1,0:T(2,128)(2,1)} %copy.22.vn_ref, bf16[16,8192,128]{2,1,0:T(8,128)(2,1)} %k_hbm.1, bf16[16,8192,128]{2,1,0:T(8,128)(2,1)} %v_hbm.1), custom_call_target="tpu_custom_call" | custom-call | tf_op jit(solution)/shard_map/attend/pallas_call | solution.py:228
  77.6 0.9 reshape.85
  78.6 0.7 copy.27
  79.3 101.6 %mlp.1 = bf16[2,4,16,1024]{3,2,1,0:T(8,128)(2,1)} custom-call(bf16[128,1024]{1,0:T(8,128)(2,1)} %get-tuple-element.12.normed, bf16[2,16,2048]{2,1,0:T(8,128)(2,1)} %bitcast.20, bf16[8,16,1024]{2,1,0:T(8,128)(2,1)} %bitcast.18, f32[1,1024]{1,0:T(1,128)} %bitcast.25, bf16[1024,8192]{1,0:T(8,128)(2,1)} %wg.1, bf16[1024,8192]{1,0:T(8,128)(2,1)} %wu.1, ...), custom_call_target="tpu_custom_call" | custom-call | tf_op jit(solution)/shard_map/mlp/pallas_call | solution.py:400
  180.8 81.8 %head.1 = (f32[128,6304]{1,0:T(8,128)}, f32[1,128]{1,0:T(1,128)}) custom-call(bf16[128,1024]{1,0:T(8,128)(2,1)} %bitcast.17, bf16[25216,1024]{1,0:T(8,128)(2,1)} %emb.1), custom_call_target="tpu_custom_call" | custom-call | tf_op jit(solution)/shard_map/head/pallas_call | solution.py:587
  262.6 2.2 broadcast_subtract_fusion
  264.9 0.0 copy-start.1
  264.9 0.0 copy-start
  264.9 0.0 copy-start.2
  264.9 2.9 %copy.24 = f32[128,6304]{0,1:T(8,128)} copy(f32[128,6304]{1,0:T(8,128)S(1)} %broadcast_subtract_fusion) | data formatting | bytes 6455296
  267.8 0.0 copy-done.1
  267.8 0.6 copy.31
  268.4 0.6 copy.32
  269.0 0.5 copy.33
  (3 shorter events, 0.0 us)
Async XLA Ops:
  264.9 2.9 %copy-start.1 = (bf16[16,128]{1,0:T(8,128)(2,1)S(1)}, bf16[16,128]{1,0:T(8,128)(2,1)}, u32[]{:S(2)}) copy-start(bf16[16,128]{1,0:T(8,128)(2,1)} %get-tuple-element.33) | copy-start | bytes 12292
  264.9 3.5 %copy-start = (bf16[16,128]{1,0:T(8,128)(2,1)S(1)}, bf16[16,128]{1,0:T(8,128)(2,1)}, u32[]{:S(2)}) copy-start(bf16[16,128]{1,0:T(8,128)(2,1)} %get-tuple-element.34) | copy-start | bytes 12292
  264.9 4.1 %copy-start.2 = (f32[1,128]{1,0:T(1,128)S(1)}, f32[1,128]{1,0:T(1,128)}, u32[]{:S(2)}) copy-start(f32[1,128]{1,0:T(1,128)} %get-tuple-element.15) | copy-start | bytes 1540

commit v2 on v1

v2 whole, which is shorter than its diff:
```python
import functools

import jax
import jax.numpy as jnp
from jax import lax
from jax.experimental import pallas as pl
from jax.experimental.pallas import tpu as pltpu
from jax.sharding import PartitionSpec as P

EPS = 1e-6
ROPE_BASE = 10000.0
MESH = pl.DeviceIdType.MESH
F32 = jnp.float32
BF16 = jnp.bfloat16
LOW = -3e38


def place():
    y = lax.axis_index("yax")
    xi = lax.axis_index("xax")
    chip = xi // 2
    core = xi % 2
    return y, xi, chip, core, chip * 2 + (1 - core), (1 - chip) * 2 + core


def send(src, dst, send_sem, recv_sem, y, xi):
    return pltpu.make_async_remote_copy(src_ref=src, dst_ref=dst, send_sem=send_sem, recv_sem=recv_sem,
                                        device_id={"yax": y, "xax": xi}, device_id_type=MESH)


def enter(peers):
    barrier = pltpu.get_barrier_semaphore()
    for y, xi in peers:
        pl.semaphore_signal(barrier, inc=1, device_id={"yax": y, "xax": xi}, device_id_type=MESH)
    return lambda: pl.semaphore_wait(barrier, len(peers))


def to_lanes(first, second):
    rows = first.shape[0]
    lane = lax.broadcasted_iota(jnp.int32, (rows, 128), 1)
    tile = jnp.where(lane == 0, first, jnp.where(lane == 1, second, 0.0))
    if rows < 128:
        tile = jnp.concatenate([tile, jnp.zeros((128 - rows, 128), F32)], axis=0)
    return tile.T[:8]


def to_columns(first, second):
    row = lax.broadcasted_iota(jnp.int32, (128, 128), 0)
    tile = jnp.where(row == 0, first, jnp.where(row == 1, second, 0.0)).T
    return tile[:, 0:1], tile[:, 1:2]


def norm_stats(values, stat, y, xi, send_sems, recv_sems, ready, size):
    rows, width = values.shape
    mean_own = jnp.sum(values, axis=1, keepdims=True) / width
    diff = values - mean_own
    stat[xi] = to_lanes(mean_own, jnp.sum(diff * diff, axis=1, keepdims=True))
    ready()
    copies = [send(stat.at[xi], stat.at[xi], send_sems.at[d - 1], recv_sems.at[d - 1], y, (xi + d) % size)
              for d in range(1, size)]
    for copy in copies:
        copy.start()
    for copy in copies:
        copy.wait()
    tiles = [stat[i] for i in range(size)]
    mean_all = sum(t[0:1] for t in tiles) / size
    spread = sum(t[1:2] for t in tiles) + width * sum((t[0:1] - mean_all) * (t[0:1] - mean_all) for t in tiles)
    mean_col, rstd_col = to_columns(mean_all, lax.rsqrt(spread / (width * size) + EPS))
    return mean_col[:rows], rstd_col[:rows]


FC = 512
RING = 4
GROUP = 4
KVS = 3


def layer_kernel(lens, hid, gain, gain_f, cos, sin, wq, wk, wv, wg, wu, wo, wd, k_hbm, v_hbm,
                 k_out, v_out, f_out,
                 n_perm, w_ring, w_kv, part_q, ga_q, sb_q, gb_q, total, q_rot, q_full, q_heads, o_heads, kn, vn,
                 part, got_a, sum_b, got_b, act, o_in, o_all, wd_ring, k_buf, v_buf, scores, probs,
                 acc, y_got, f_all, stat, stat_f,
                 w_sem, kv_sem, wd_sem, k_sem, v_sem, a_s, a_r, b_s, b_r, m_s, m_r, p_s, p_r,
                 q_s, q_r, o_s, o_r, st_s, st_r, sf_s, sf_r):
    y, xi, chip, core, partner, twin = place()
    width = n_perm.shape[1]
    qc, hd = wq.shape[1], wk.shape[1]
    heads = qc // hd
    steps = part.shape[0]
    groups = act.shape[0]
    seqs = q_heads.shape[0]
    length = k_buf.shape[1]
    mine = y * 4 + xi
    ready = enter([(y, (xi + d) % 4) for d in (1, 2, 3)] + [(1 - y, xi)])

    def q_loads(s):
        return [pltpu.make_async_copy(wq.at[:, pl.ds((2 * s + i) * FC, FC)], w_ring.at[s, i], w_sem.at[s, i])
                for i in range(2)]

    def w_loads(j):
        cols = pl.ds(pl.multiple_of(j * FC, FC), FC)
        slot = (j + 2) % RING
        return [pltpu.make_async_copy(w.at[:, cols], w_ring.at[slot, i], w_sem.at[slot, i])
                for i, w in enumerate((wg, wu))]

    def start(copies):
        for copy in copies:
            copy.start()

    kv_w = [pltpu.make_async_copy(w, w_kv.at[:, pl.ds(i * hd, hd)], kv_sem.at[i]) for i, w in enumerate((wk, wv))]
    start(q_loads(0))
    start(q_loads(1))
    start(kv_w)
    start(w_loads(0))

    def cache_loads(b):
        slot = b % KVS
        return [pltpu.make_async_copy(k_hbm.at[b], k_buf.at[slot], k_sem.at[slot]),
                pltpu.make_async_copy(v_hbm.at[b], v_buf.at[slot], v_sem.at[slot])]

    def wd_load(g):
        src = wo if g == groups else wd.at[pl.ds(g * GROUP * FC, GROUP * FC)]
        return pltpu.make_async_copy(src, wd_ring.at[g % 2], wd_sem.at[g % 2])

    def hop_a(j):
        return send(part.at[j, 1 - core], got_a.at[j], a_s.at[j], a_r.at[j], y, partner)

    def hop_b(j):
        return send(sum_b.at[j], got_b.at[j], b_s.at[j], b_r.at[j], y, twin)

    def hop_m(g):
        return send(act.at[g, core, chip], act.at[g, core, chip], m_s.at[g], m_r.at[g], y, twin)

    def hop_p(g):
        return send(act.at[g, core], act.at[g, core], p_s.at[g], p_r.at[g], y, partner)

    hop_qa = send(part_q.at[1 - core], ga_q, q_s.at[0], q_r.at[0], y, partner)
    hop_qb = send(sb_q, gb_q, q_s.at[1], q_r.at[1], y, twin)
    hop_qc = send(q_rot.at[1 - y], q_full.at[y], q_s.at[2], q_r.at[2], 1 - y, xi)
    hop_o0 = send(o_in.at[1 - y], o_all.at[core, chip, y], o_s.at[0], o_r.at[0], 1 - y, xi)
    hop_o1 = send(o_all.at[core, chip], o_all.at[core, chip], o_s.at[1], o_r.at[1], y, twin)
    hop_o2 = send(o_all.at[core], o_all.at[core], o_s.at[2], o_r.at[2], y, partner)
    hop_y = send(acc.at[:, 1 - y], y_got, o_s.at[3], o_r.at[3], 1 - y, xi)
    hop_f = send(f_all.at[y], f_all.at[y], o_s.at[4], o_r.at[4], 1 - y, xi)

    h = hid[...].astype(F32).reshape(128, width)
    mean, rstd = norm_stats(h, stat, y, xi, st_s, st_r, ready, 4)
    normed = ((h - mean) * rstd * gain[...]).astype(BF16)
    for core_o in range(2):
        for chip_o in range(2):
            for y_o in range(2):
                src = (y_o * 4 + chip_o * 2 + core_o) * 16
                dst = (core_o * 4 + chip_o * 2 + y_o) * 16
                n_perm[dst:dst + 16, :] = normed[src:src + 16, :]

    for s in range(2):
        for i, load in enumerate(q_loads(s)):
            load.wait()
            prod = jnp.dot(n_perm[...], w_ring[s, i], preferred_element_type=F32)
            part_q[:, :, :, (2 * s + i) * FC:(2 * s + i + 1) * FC] = prod.reshape(2, 2, 32, FC)
        start(w_loads(s + 1))
    for load in kv_w:
        load.wait()
    part_q[:, :, :, qc:] = jnp.dot(n_perm[...], w_kv[...], preferred_element_type=F32).reshape(2, 2, 32, 2 * hd)
    hop_qa.start()

    def rotate_queries():
        hop_qb.wait_recv()
        both = part_q[core, chip] + ga_q[chip] + gb_q[...]
        total[...] = both.astype(BF16).astype(F32).reshape(2, 16, qc + 2 * hd)
        for y_o in range(2):
            block = y_o * 4 + chip * 2 + core
            cos_r, sin_r = cos[block], sin[block]
            for head in range(heads):
                val = total[y_o, :, head * hd:(head + 1) * hd]
                q_rot[y_o, :, head * hd:(head + 1) * hd] = (val * cos_r + pltpu.roll(val, hd // 2, 1) * sin_r).astype(BF16)
        hop_qc.start()
        key = total[y, :, qc:qc + hd]
        key = (key * cos[mine] + pltpu.roll(key, hd // 2, 1) * sin[mine]).astype(BF16)
        k_out[...] = key
        v_out[...] = total[y, :, qc + hd:].astype(BF16)
        kn[:, 0, :] = key.astype(F32)
        vn[:, 0, :] = total[y, :, qc + hd:]
        q_full[y] = q_rot[y]

    def spread_queries():
        hop_qc.wait_recv()
        for y_o in range(2):
            for head in range(heads):
                q_heads[:, y_o * heads + head, :] = q_full[y_o, :, head * hd:(head + 1) * hd].astype(F32)

    def add_pair(j):
        hop_a(j).wait_recv()
        sum_b[j] = part[j, core, 1 - chip] + got_a[j, 1 - chip]
        hop_b(j).start()

    def project(j, carry):
        @pl.when(j + 3 < steps)
        def _():
            start(w_loads(j + 3))

        slot = (j + 2) % RING
        for i, load in enumerate(w_loads(j)):
            load.wait()
            prod = jnp.dot(n_perm[...], w_ring[slot, i], preferred_element_type=F32)
            part[j, :, :, :, i * FC:(i + 1) * FC] = prod.reshape(2, 2, 32, FC)
        hop_a(j).start()

        @pl.when(j == 0)
        def _():
            hop_qa.wait_recv()
            sb_q[...] = part_q[core, 1 - chip] + ga_q[1 - chip]
            hop_qb.start()

        @pl.when(j >= 1)
        def _():
            add_pair(j - 1)

        @pl.when(j == 4)
        def _():
            for b in range(KVS):
                start(cache_loads(b))

        @pl.when(j == 8)
        def _():
            rotate_queries()

        @pl.when(j == 12)
        def _():
            spread_queries()
        return carry

    lax.fori_loop(0, steps, project, 0)
    add_pair(steps - 1)
    wd_load(0).start()
    wd_load(1).start()

    def activate(j):
        hop_b(j).wait_recv()
        both = part[j, core, chip] + got_a[j, chip] + got_b[j]
        gate = both[:, :FC].astype(BF16).astype(F32)
        up_val = both[:, FC:].astype(BF16).astype(F32)
        cols = pl.ds(pl.multiple_of((j % GROUP) * FC, FC), FC)
        act[j // GROUP, core, chip, :, cols] = (jax.nn.silu(gate) * up_val).astype(BF16)

        @pl.when(j % GROUP == GROUP - 1)
        def _():
            hop_m(j // GROUP).start()

    part_len = 1024

    def attend(b):
        slot = b % KVS
        scale = hd ** -0.5
        q32 = q_heads[b]
        q = q32.astype(BF16)
        limit = lens[mine * 16 + b]
        s_new = jnp.sum(q32 * kn[b], axis=1, keepdims=True) * scale
        load_k, load_v = cache_loads(b)
        load_k.wait()
        high = None
        for i in range(length // part_len):
            rows = slice(i * part_len, (i + 1) * part_len)
            s = lax.dot_general(q, k_buf[slot, rows], (((1,), (1,)), ((), ())), preferred_element_type=F32) * scale
            pos = lax.broadcasted_iota(jnp.int32, s.shape, 1) + i * part_len
            s = jnp.where(pos < limit, s, -jnp.inf)
            scores[:, rows] = s
            for c in range(0, part_len, 128):
                high = s[:, c:c + 128] if high is None else jnp.maximum(high, s[:, c:c + 128])
        top = jnp.maximum(jnp.max(high, axis=1, keepdims=True), s_new)
        mass = None
        for i in range(length // part_len):
            rows = slice(i * part_len, (i + 1) * part_len)
            e = jnp.exp(scores[:, rows] - top)
            scores[:, rows] = e
            for c in range(0, part_len, 128):
                mass = e[:, c:c + 128] if mass is None else mass + e[:, c:c + 128]
        e_new = jnp.exp(s_new - top)
        inv = 1.0 / (jnp.sum(mass, axis=1, keepdims=True) + e_new)
        for i in range(length // part_len):
            rows = slice(i * part_len, (i + 1) * part_len)
            probs[:, rows] = (scores[:, rows] * inv).astype(BF16)
        load_v.wait()
        o = jnp.dot(probs[...], v_buf[slot], preferred_element_type=F32)
        o = o + (e_new * inv).astype(BF16).astype(F32) * vn[b]
        o_heads[b] = o.astype(BF16).astype(F32)

        @pl.when(b + KVS < seqs)
        def _():
            start(cache_loads(b + KVS))

    def mix(j, carry):
        attend(j)
        activate(j)
        return carry

    lax.fori_loop(0, steps, mix, 0)
    for y_o in range(2):
        for head in range(heads):
            o_in[y_o, :, head * hd:(head + 1) * hd] = o_heads[:, y_o * heads + head, :].astype(BF16)
    o_all[core, chip, y] = o_in[y]
    hop_o0.start()
    for g in range(groups + 1):
        if g < groups:
            hop_m(g).wait_recv()
            hop_p(g).start()
            if g == 0:
                hop_o0.wait_recv()
                hop_o1.start()
            hop_p(g).wait_recv()
            left = act[g].reshape(128, GROUP * FC)
        else:
            hop_o1.wait_recv()
            hop_o2.start()
            hop_o2.wait_recv()
            left = o_all[...].reshape(128, qc)
        wd_load(g).wait()
        prod = jnp.dot(left, wd_ring[g % 2], preferred_element_type=F32).reshape(acc.shape)
        acc[...] = prod if g == 0 else acc[...] + prod
        if g + 2 <= groups:
            wd_load(g + 2).start()

    hop_y.start()
    hop_y.wait_recv()
    res = [hid[y * 4 + (i % 2) * 2 + i // 2].astype(F32) for i in range(4)]
    branch = acc[:, y] + y_got[...]
    r = jnp.concatenate(res, axis=0) + branch.reshape(64, width)
    mean, rstd = norm_stats(r, stat_f, y, xi, sf_s, sf_r, lambda: None, 4)
    f = ((r - mean) * rstd * gain_f[...]).astype(BF16)
    for i in range(4):
        f_all[y, (i % 2) * 2 + i // 2] = f[i * 16:(i + 1) * 16]
    hop_f.start()
    f_out[y] = f_all[y]
    hop_f.wait_recv()
    f_out[1 - y] = f_all[1 - y]

    def drain(j, carry):
        hop_a(j).wait_send()
        hop_b(j).wait_send()
        return carry

    lax.fori_loop(0, steps, drain, 0)
    for g in range(groups):
        hop_m(g).wait_send()
        hop_p(g).wait_send()
    for hop in (hop_qa, hop_qb, hop_qc, hop_o0, hop_o1, hop_o2, hop_y, hop_f):
        hop.wait_send()


def layer_call(lens, hid, gain, gain_f, cos, sin, wq, wk, wv, wg, wu, wo, wd, k_cache, v_cache):
    width = hid.shape[2]
    qc, hd = wq.shape[1], wk.shape[1]
    seqs, length, _ = k_cache.shape
    cols = qc + 2 * hd
    steps = wg.shape[1] // FC
    heads = 2 * qc // hd
    vmem = pl.BlockSpec(memory_space=pltpu.VMEM)
    hbm = pl.BlockSpec(memory_space=pl.ANY)
    dma = pltpu.SemaphoreType.DMA

    def f32(*shape):
        return pltpu.VMEM(shape, F32)

    def bf16(*shape):
        return pltpu.VMEM(shape, BF16)

    return pl.pallas_call(
        layer_kernel, name="layer",
        out_shape=[jax.ShapeDtypeStruct((16, hd), BF16), jax.ShapeDtypeStruct((16, hd), BF16),
                   jax.ShapeDtypeStruct((2, 4, 16, width), BF16)],
        in_specs=[pl.BlockSpec(memory_space=pltpu.SMEM)] + [vmem] * 5 + [hbm] * 9, out_specs=[vmem] * 3,
        scratch_shapes=[
            bf16(128, width), bf16(RING, 2, width, FC), bf16(width, 2 * hd),
            f32(2, 2, 32, cols), f32(2, 32, cols), f32(32, cols), f32(32, cols), f32(2, 16, cols),
            bf16(2, 16, qc), bf16(2, 16, qc), f32(seqs, heads, hd), f32(seqs, heads, hd), f32(seqs, 1, hd), f32(seqs, 1, hd),
            f32(steps, 2, 2, 32, 2 * FC), f32(steps, 2, 32, 2 * FC), f32(steps, 32, 2 * FC), f32(steps, 32, 2 * FC),
            bf16(steps // GROUP, 2, 2, 32, GROUP * FC), bf16(2, 16, qc), bf16(2, 2, 2, 16, qc), bf16(2, GROUP * FC, width),
            bf16(KVS, length, hd), bf16(KVS, length, hd), f32(heads, length), bf16(heads, length),
            f32(4, 2, 16, width), f32(4, 16, width), bf16(2, 4, 16, width), f32(4, 8, 128), f32(4, 8, 128),
            dma((RING, 2)), dma((2,)), dma((2,)), dma((KVS,)), dma((KVS,))] + [dma((steps,))] * 4
        + [dma((steps // GROUP,))] * 4 + [dma((3,))] * 2 + [dma((5,))] * 2 + [dma((3,))] * 4,
        compiler_params=pltpu.CompilerParams(collective_id=0, has_side_effects=True, vmem_limit_bytes=63 * 2**20),
    )(lens, hid, gain, gain_f, cos, sin, wq, wk, wv, wg, wu, wo, wd, k_cache, v_cache)


VC = 512
ERING = 8


def head_kernel(share, f_ref, emb, z_out, lse_out,
                e_ring, e_tail, buf_a, buf_b, buf_c, buf_d, got_a, got_b, got_c,
                t_a, t_b, t_c, t_d, tg_a, tg_b, tg_c, top, total, stat,
                e_sem, tail_sem, a_s, a_r, b_s, b_r, c_s, c_r, t_s, t_r, stat_s, stat_r):
    y, xi, chip, core, partner, twin = place()
    full = share // VC
    rest = share - full * VC
    tail = full * VC
    ready = enter([(y, (xi + d) % 4) for d in (1, 2, 3)] + [(1 - y, (xi + d) % 4) for d in range(4)])
    far = (1 - chip) * 2
    near = chip * 2

    def share_of(i):
        side = i // 2
        mine = i % 2
        base = far + side * (near - far)
        return base + (1 - core) + mine * (2 * core - 1)

    def e_load(t):
        k = (t // 2) % full
        i = (t // (2 * full)) * 2 + t % 2
        rows = pl.ds(pl.multiple_of(share_of(i) * share + k * VC, 32), VC)
        return pltpu.make_async_copy(emb.at[rows], e_ring.at[t % ERING], e_sem.at[t % ERING])

    def tail_load(i):
        rows = pl.ds(pl.multiple_of(share_of(i) * share + tail, 32), rest)
        return pltpu.make_async_copy(emb.at[rows], e_tail.at[i], tail_sem.at[i])

    for i in range(4):
        tail_load(i).start()
    for t in range(ERING - 1):
        e_load(t).start()

    def hop_a(k):
        return send(buf_a.at[k], got_a.at[k], a_s.at[k], a_r.at[k], y, partner)

    def hop_b(k):
        return send(buf_b.at[k], got_b.at[k], b_s.at[k], b_r.at[k], y, twin)

    def hop_c(k):
        return send(buf_c.at[k], got_c.at[k], c_s.at[k], c_r.at[k], y, partner)

    hop_ta = send(t_a, tg_a, t_s.at[0], t_r.at[0], y, partner)
    hop_tb = send(t_b, tg_b, t_s.at[1], t_r.at[1], y, twin)
    hop_tc = send(t_c, tg_c, t_s.at[2], t_r.at[2], y, partner)

    def product(e):
        return lax.dot_general(f_ref[...], e, (((1,), (1,)), ((), ())), preferred_element_type=F32)

    for t_ref in (t_a, t_b, t_c, t_d):
        t_ref[...] = jnp.zeros_like(t_ref)

    def tail_product(i, t_ref):
        tail_load(i).wait()
        t_ref[:, :rest] = product(e_tail[i])

    def chunk_product(t, buf, k):
        @pl.when(t + ERING - 1 < 4 * full)
        def _():
            e_load(t + ERING - 1).start()

        e_load(t).wait()
        buf[k] = product(e_ring[t % ERING])

    tail_product(0, t_a)
    ready()
    hop_ta.start()
    tail_product(1, t_b)
    hop_ta.wait_recv()
    t_b[...] += tg_a[...]
    hop_tb.start()

    def add_pair(k):
        hop_a(k).wait_recv()
        buf_b[k] += got_a[k]
        hop_b(k).start()

    def outward(k, carry):
        chunk_product(2 * k, buf_a, k)
        hop_a(k).start()
        chunk_product(2 * k + 1, buf_b, k)

        @pl.when(k >= 1)
        def _():
            add_pair(k - 1)
        return carry

    lax.fori_loop(0, full, outward, 0)
    add_pair(full - 1)
    tail_product(2, t_c)
    hop_tc.start()
    tail_product(3, t_d)

    def inward(k, carry):
        chunk_product(2 * full + 2 * k, buf_c, k)
        hop_c(k).start()
        chunk_product(2 * full + 2 * k + 1, buf_d, k)
        return carry

    lax.fori_loop(0, full, inward, 0)

    top[...] = jnp.full_like(top, LOW)
    total[...] = jnp.zeros_like(total)

    def fold(z):
        groups = [z[:, i:i + 128] for i in range(0, z.shape[1], 128)]
        high = functools.reduce(jnp.maximum, groups, top[...])
        total[...] = total[...] * jnp.exp(top[...] - high) + sum(jnp.exp(g - high) for g in groups)
        top[...] = high

    hop_tc.wait_recv()
    hop_tb.wait_recv()
    z_tail = t_d[...] + tg_c[...] + tg_b[...]
    z_out[:, tail:] = z_tail[:, :rest]
    lane = lax.broadcasted_iota(jnp.int32, z_tail.shape, 1)
    fold(jnp.where(lane < rest, z_tail, LOW))

    def finish(k, carry):
        hop_c(k).wait_recv()
        hop_b(k).wait_recv()
        z = buf_d[k] + got_c[k] + got_b[k]
        z_out[:, pl.ds(pl.multiple_of(k * VC, VC), VC)] = z
        fold(z)
        return carry

    lax.fori_loop(0, full, finish, 0)
    high = jnp.max(top[...], axis=1, keepdims=True)
    mass = jnp.sum(total[...] * jnp.exp(top[...] - high), axis=1, keepdims=True)
    me = y * 4 + xi
    stat[me] = to_lanes(high, mass)
    copies = []
    for dy in range(2):
        for d in range(4):
            if dy or d:
                i = dy * 4 + d - 1
                copies.append(send(stat.at[me], stat.at[me], stat_s.at[i], stat_r.at[i],
                                   y + dy * (1 - 2 * y), (xi + d) % 4))
    for copy in copies:
        copy.start()
    for copy in copies:
        copy.wait()
    highs = [stat[i][0:1] for i in range(8)]
    best = functools.reduce(jnp.maximum, highs)
    mass_all = sum(stat[i][1:2] * jnp.exp(highs[i] - best) for i in range(8))
    lse_out[...] = best + jnp.log(mass_all)

    def drain(k, carry):
        hop_a(k).wait_send()
        hop_b(k).wait_send()
        hop_c(k).wait_send()
        return carry

    lax.fori_loop(0, full, drain, 0)
    for hop in (hop_ta, hop_tb, hop_tc):
        hop.wait_send()


def head_call(f, emb):
    rows, width = f.shape
    share = emb.shape[0] // 4
    full = share // VC
    rest = share - full * VC
    vmem = pl.BlockSpec(memory_space=pltpu.VMEM)
    hbm = pl.BlockSpec(memory_space=pl.ANY)
    dma = pltpu.SemaphoreType.DMA
    tail_w = -(-rest // 128) * 128
    return pl.pallas_call(
        functools.partial(head_kernel, share), name="head",
        out_shape=[jax.ShapeDtypeStruct((rows, share), F32), jax.ShapeDtypeStruct((1, rows), F32)],
        in_specs=[vmem, hbm], out_specs=[vmem, vmem],
        scratch_shapes=[pltpu.VMEM((ERING, VC, width), BF16), pltpu.VMEM((4, rest, width), BF16)]
        + [pltpu.VMEM((full, rows, VC), F32)] * 7 + [pltpu.VMEM((rows, tail_w), F32)] * 7
        + [pltpu.VMEM((rows, 128), F32)] * 2 + [pltpu.VMEM((8, 8, 128), F32)]
        + [dma((ERING,)), dma((4,))] + [dma((full,))] * 6 + [dma((3,))] * 2 + [dma((7,))] * 2,
        compiler_params=pltpu.CompilerParams(collective_id=1, has_side_effects=True, vmem_limit_bytes=60 * 2**20),
    )(f, emb)


def solution(mesh):
    row_spec = P(("dp", "yax", "xax"))

    def local_step(hidden, cache_len, k_cache, v_cache, g_attn, w_query, w_key, w_value,
                   w_gate, w_up, w_out, w_down, g_final, embedding):
        rows, width = hidden.shape
        own_rows, _, head_dim = k_cache.shape
        half = head_dim // 2
        inv_freq = ROPE_BASE ** (-(jnp.arange(half, dtype=F32) * 2.0) / head_dim)
        angles = cache_len.astype(F32)[:, None] * inv_freq[None, :]
        cos_a, sin_a = jnp.cos(angles), jnp.sin(angles)
        cos_t = jnp.concatenate([cos_a, cos_a], axis=1).reshape(8, own_rows, head_dim)
        sin_t = jnp.concatenate([-sin_a, sin_a], axis=1).reshape(8, own_rows, head_dim)

        key_own, value_own, f = layer_call(cache_len, hidden.reshape(8, own_rows, width), g_attn[None], g_final[None], cos_t, sin_t,
                                           w_query, w_key, w_value, w_gate, w_up, w_out, w_down, k_cache, v_cache)
        logits, log_norm = head_call(f.reshape(rows, width), embedding)
        log_norm = log_norm[0]
        return key_own, value_own, logits - log_norm[:, None], log_norm

    in_specs = (P("dp", "xax"), P("dp"), row_spec, row_spec, P("xax"), P("xax", "yax"),
                P("xax", None), P("xax", None), P("xax", "yax"), P("xax", "yax"),
                P("yax", "xax"), P("yax", "xax"), P("xax"), P("yax", "xax"))
    out_specs = (row_spec, row_spec, P("dp", ("yax", "xax")), P("dp"))
    return jax.shard_map(local_step, mesh=mesh, in_specs=in_specs, out_specs=out_specs, check_vma=False)
```

time: 273 us -> 189 us (0.69); the launches traced: 269 us -> 189 us
  Pallas kernels: 253 us -> 180 us
  local copies, waits for them, and re-layouts: 11.7 us -> 4.69 us
    pallas_call x3 -> x1, Pallas kernels: 171 us -> 98.2 us  [layer_call(): pl.pallas_call(layer_kernel, name='layer', out_shape=[jax.ShapeDtypeStruc...]
    reshape x5 -> x0, local copies, waits for them, and re-layouts: 4.85 us -> none  [the longest x2 1.64 us: local_step(): attn = attn.reshape(own_rows, 2, half_heads * head_dim).transpose(1, 0, 2)]
    unnamed x11 -> x10, local copies, waits for them, and re-layouts: 5.54 us -> 4.61 us
where the time goes in v2:
time: 189 us
  Pallas kernels  180 us (95%)
  local copies, waits for them, and re-layouts  4.69 us (2%)
  other arithmetic  3.95 us (2%)
    pallas_call x1, Pallas kernels, layer_call(): pl.pallas_call(layer_kernel, name='layer', out_shape=[jax.ShapeDtypeStruc...  98.2 us
    pallas_call x1, Pallas kernels, head_call(): pl.pallas_call(functools.partial(head_kernel, share), name='head', out_sh...  81.8 us
    unnamed x10, local copies, waits for them, and re-layouts  4.61 us

profile of v2, /device:TPU:0, one launch (start us, length us, event | category | flops | bytes accessed | tf_op | source)
XLA Modules:
  0.0 189.3 jit_solution(12508137103829944398)
XLA Ops:
  0.6 0.7 convert_element_type.3
  1.3 0.1 mul.29
  1.4 0.3 fusion
  1.7 0.8 pad_maximum_fusion
  2.5 98.2 %layer.1 = (bf16[16,128]{1,0:T(8,128)(2,1)}, bf16[16,128]{1,0:T(8,128)(2,1)}, bf16[2,4,16,1024]{3,2,1,0:T(8,128)(2,1)}) custom-call(s32[128]{0:T(128)} %lens.1, bf16[8,16,1024]{2,1,0:T(8,128)(2,1)} %bitcast.5, f32[1,1024]{1,0:T(1,128)} %bitcast.7, f32[1,1024]{1,0:T(1,128)} %bitcast.8, f32[8,16,128]{2,1,0:T(8,128)} %get-tuple-element.21.cos, ...), custom_call_target="tpu_custom_call" | custom-call | tf_op jit(solution)/shard_map/layer/pallas_call | solution.py:367
  100.6 81.8 %head.1 = (f32[128,6304]{1,0:T(8,128)}, f32[1,128]{1,0:T(1,128)}) custom-call(bf16[128,1024]{1,0:T(8,128)(2,1)} %bitcast.6, bf16[25216,1024]{1,0:T(8,128)(2,1)} %emb.1), custom_call_target="tpu_custom_call" | custom-call | tf_op jit(solution)/shard_map/head/pallas_call | solution.py:556
  182.5 2.2 %broadcast_subtract_fusion = f32[128,6304]{1,0:T(8,128)S(1)} fusion(f32[128,6304]{1,0:T(8,128)} %get-tuple-element.12, f32[128]{0:T(128)} %bitcast.9), kind=kLoop, calls=%fused_computation | loop fusion | flops 806912 | bytes 6455808 | tf_op jit(solution)/shard_map/sub | solution.py:586
  184.7 0.0 copy-start.1
  184.7 0.0 copy-start
  184.7 0.0 copy-start.2
  184.7 2.9 %copy.18 = f32[128,6304]{0,1:T(8,128)} copy(f32[128,6304]{1,0:T(8,128)S(1)} %broadcast_subtract_fusion) | data formatting | bytes 6455296
  187.6 0.0 copy-done.1
  187.6 0.6 copy.22
  188.2 0.0 copy-done
  188.2 0.6 copy.23
  188.8 0.0 copy-done.2
  188.8 0.5 copy.24
  (1 shorter events, 0.0 us)
Async XLA Ops:
  184.7 2.9 %copy-start.1 = (bf16[16,128]{1,0:T(8,128)(2,1)S(1)}, bf16[16,128]{1,0:T(8,128)(2,1)}, u32[]{:S(2)}) copy-start(bf16[16,128]{1,0:T(8,128)(2,1)} %get-tuple-element.27) | copy-start | bytes 12292
  184.7 3.5 %copy-start = (bf16[16,128]{1,0:T(8,128)(2,1)S(1)}, bf16[16,128]{1,0:T(8,128)(2,1)}, u32[]{:S(2)}) copy-start(bf16[16,128]{1,0:T(8,128)(2,1)} %get-tuple-element.28) | copy-start | bytes 12292
  184.7 4.1 %copy-start.2 = (f32[1,128]{1,0:T(1,128)S(1)}, f32[1,128]{1,0:T(1,128)}, u32[]{:S(2)}) copy-start(f32[1,128]{1,0:T(1,128)} %get-tuple-element.13) | copy-start | bytes 1540

commit v3 on v0

v3 whole, which is shorter than its diff:
```python
import functools

import jax
import jax.numpy as jnp
from jax import lax
from jax.experimental import pallas as pl
from jax.experimental.pallas import tpu as pltpu
from jax.sharding import PartitionSpec as P

EPS = 1e-6
ROPE_BASE = 10000.0
MESH = pl.DeviceIdType.MESH
F32 = jnp.float32
BF16 = jnp.bfloat16
LOW = -3e38
TWO, QUAD, OCT, OWN, PAIR, HALF, LANES = 2, 4, 8, 16, 32, 64, 128


def place():
    y = lax.axis_index("yax")
    xi = lax.axis_index("xax")
    chip = xi // 2
    core = xi % 2
    return y, xi, chip, core, chip * 2 + (1 - core), (1 - chip) * 2 + core


def send(src, dst, send_sem, recv_sem, y, xi):
    return pltpu.make_async_remote_copy(src_ref=src, dst_ref=dst, send_sem=send_sem, recv_sem=recv_sem,
                                        device_id={"yax": y, "xax": xi}, device_id_type=MESH)


def enter(peers):
    barrier = pltpu.get_barrier_semaphore()
    for y, xi in peers:
        pl.semaphore_signal(barrier, inc=1, device_id={"yax": y, "xax": xi}, device_id_type=MESH)
    return lambda: pl.semaphore_wait(barrier, len(peers))


def to_lanes(first, second):
    rows = first.shape[0]
    lane = lax.broadcasted_iota(jnp.int32, (rows, 128), 1)
    tile = jnp.where(lane == 0, first, jnp.where(lane == 1, second, 0.0))
    if rows < 128:
        tile = jnp.concatenate([tile, jnp.zeros((128 - rows, 128), F32)], axis=0)
    return tile.T[:8]


def to_columns(first, second):
    row = lax.broadcasted_iota(jnp.int32, (128, 128), 0)
    tile = jnp.where(row == 0, first, jnp.where(row == 1, second, 0.0)).T
    return tile[:, 0:1], tile[:, 1:2]


def norm_stats(values, stat, y, xi, send_sems, recv_sems, ready, size, after=lambda: None):
    rows, width = values.shape
    mean_own = jnp.sum(values, axis=1, keepdims=True) / width
    diff = values - mean_own
    stat[xi] = to_lanes(mean_own, jnp.sum(diff * diff, axis=1, keepdims=True))
    ready()
    copies = [send(stat.at[xi], stat.at[xi], send_sems.at[d - 1], recv_sems.at[d - 1], y, (xi + d) % size)
              for d in range(1, size)]
    for copy in copies:
        copy.start()
    after()
    for copy in copies:
        copy.wait()
    tiles = [stat[i] for i in range(size)]
    mean_all = sum(t[0:1] for t in tiles) / size
    spread = sum(t[1:TWO] for t in tiles) + width * sum((t[0:1] - mean_all) * (t[0:1] - mean_all) for t in tiles)
    mean_col, rstd_col = to_columns(mean_all, lax.rsqrt(spread / (width * size) + EPS))
    return mean_col[:rows], rstd_col[:rows]


FC = 512
WB = 1024
RING = 6
KVS = 3
HELD = 5


def step_kernel(lens, hid_h, gain_h, gain_fh, freq, wq, wk, wv, wg, wu, wo, wd, emb, k_hbm, v_hbm,
                kv_out, z_out, lse_out,
                hid, gain, gain_f, cos, sin, n_perm, ring, w_kv, part_q, ga_q, sb_q, gb_q, total, q_rot, q_full, q_heads, o_heads, kn, vn,
                pool, act, o_in, o_all, k_buf, v_buf, scores, probs, acc, y_got, f_all, f_nat, e_tail,
                t_a, t_b, tg_a, tg_b, t_c, tg_c, top, mass_l, stat, stat_f, stat_z,
                i_sem, r_sem, kv_sem, tail_sem, k_sem, v_sem, a_s, a_r, b_s, b_r, m_s, m_r, p_s, p_r, q_s, q_r,
                o_s, o_r, y_s, y_r, f_s, f_r, st_s, st_r, sf_s, sf_r,
                la_s, la_r, lb_s, lb_r, lc_s, lc_r, ta_s, ta_r, tb_s, tb_r, tc_s, tc_r, sz_s, sz_r):
    y, xi, chip, core, partner, twin = place()
    width = n_perm.shape[1]
    hw = width // TWO
    qc, hd = wq.shape[1], wk.shape[1]
    heads = qc // hd
    steps = wg.shape[1] // FC
    seqs = q_heads.shape[0]
    length = k_buf.shape[1]
    share = emb.shape[0] // 4
    full = share // WB
    rest = share - full * WB
    mine = y * 4 + xi
    ready = enter([(y, (xi + d) % 4) for d in (1, TWO, 3)] + [(1 - y, (xi + d) % 4) for d in range(4)])

    def start(copies):
        for copy in copies:
            copy.start()

    def q_loads(s):
        return [pltpu.make_async_copy(wq.at[:, pl.ds((TWO * s + i) * FC, FC)], ring.at[s, i], r_sem.at[s, i]) for i in range(TWO)]

    def w_loads(j):
        cols = pl.ds(pl.multiple_of(j * FC, FC), FC)
        slot = (j + TWO) % RING
        return [pltpu.make_async_copy(w.at[:, cols], ring.at[slot, i], r_sem.at[slot, i]) for i, w in enumerate((wg, wu))]

    inputs = [pltpu.make_async_copy(src, dst, i_sem.at[i])
              for i, (src, dst) in enumerate(((hid_h, hid), (gain_h, gain), (gain_fh, gain_f)))]
    start(inputs)
    kv_w = [pltpu.make_async_copy(w, w_kv.at[:, pl.ds(i * hd, hd)], kv_sem.at[i]) for i, w in enumerate((wk, wv))]
    start(q_loads(0))
    start(q_loads(1))
    start(kv_w)
    for j in range(RING - 3):
        start(w_loads(j))

    nd, no = wd.shape[0] // WB, wo.shape[0] // WB
    np_ = nd + no
    e_base = (np_, TWO * np_ + TWO * full)
    c_base = TWO * np_ + 4 * full
    d_base = c_base + full
    items = d_base + full
    far, near = (1 - chip) * TWO, chip * TWO

    def block(src, row, t):
        slot = t % RING
        return [pltpu.make_async_copy(src.at[pl.ds(row, WB), pl.ds(i * hw, hw)], ring.at[slot, i], r_sem.at[slot, i])
                for i in range(TWO)]

    def emb_row(quarter, k):
        return pl.multiple_of(quarter * share + k * WB, PAIR)

    def load_item(t):
        for base in (0, np_ + TWO * full):
            @pl.when((t >= base) & (t < base + nd))
            def _(base=base):
                start(block(wd, pl.multiple_of((t - base) * WB, WB), t))

            @pl.when((t >= base + nd) & (t < base + np_))
            def _(base=base):
                start(block(wo, pl.multiple_of((t - base - nd) * WB, WB), t))

        for base in e_base:
            @pl.when((t >= base) & (t < base + TWO * full))
            def _(base=base):
                k, own = (t - base) // TWO, (t - base) % TWO
                start(block(emb, emb_row(far + (1 - core) + own * (TWO * core - 1), k), t))

        @pl.when((t >= c_base) & (t < d_base))
        def _():
            start(block(emb, emb_row(near + 1 - core, t - c_base), t))

        @pl.when((t >= d_base) & (t < items))
        def _():
            start(block(emb, emb_row(near + core, t - d_base), t))

    def take_item(t):
        load_item(t + RING - 1)
        for copy in block(wd, 0, t):
            copy.wait()
        return t % RING

    def tail_load(i):
        quarter = (far + 1 - core, far + core, near + 1 - core, near + core)[i]
        rows = pl.ds(pl.multiple_of(quarter * share + full * WB, PAIR), rest)
        return pltpu.make_async_copy(emb.at[rows], e_tail.at[i], tail_sem.at[i])

    def cache_loads(b):
        slot = b % KVS
        return [pltpu.make_async_copy(k_hbm.at[b], k_buf.at[slot], k_sem.at[slot]),
                pltpu.make_async_copy(v_hbm.at[b], v_buf.at[slot], v_sem.at[slot])]

    def hop_a(j):
        return send(pool.at[pl.ds(TWO * j, TWO), 1 - core], pool.at[TWO * steps + j], a_s.at[j], a_r.at[j], y, partner)

    def sum_at(hf, p):
        return pool.at[3 * steps + hf * (steps // 4) + p // TWO, p % TWO]

    def got_at(hf, p):
        return pool.at[3 * steps + (TWO + hf) * (steps // 4) + p // TWO, p % TWO]

    def hop_b(hf, p):
        return send(sum_at(hf, p), got_at(hf, p), b_s.at[hf, p], b_r.at[hf, p], y, twin)

    def hop_m(hf, g):
        return send(act.at[hf, g, core, chip], act.at[hf, g, core, chip], m_s.at[hf, g], m_r.at[hf, g], y, twin)

    def hop_p(hf, g):
        return send(act.at[hf, g, core], act.at[hf, g, core], p_s.at[hf, g], p_r.at[hf, g], y, partner)

    hop_qa = send(part_q.at[:, 1 - core], ga_q, q_s.at[0], q_r.at[0], y, partner)
    hop_qb = send(sb_q, gb_q, q_s.at[1], q_r.at[1], y, twin)
    hop_qc = send(q_rot.at[1 - y], q_full.at[y], q_s.at[TWO], q_r.at[TWO], 1 - y, xi)

    def hop_o(hf, n):
        if n == 0:
            return send(o_in.at[1 - y, hf], o_all.at[hf, core, chip, y], o_s.at[hf, 0], o_r.at[hf, 0], 1 - y, xi)
        if n == 1:
            return send(o_all.at[hf, core, chip], o_all.at[hf, core, chip], o_s.at[hf, 1], o_r.at[hf, 1], y, twin)
        return send(o_all.at[hf, core], o_all.at[hf, core], o_s.at[hf, TWO], o_r.at[hf, TWO], y, partner)

    def hop_y(hf):
        return send(acc.at[hf, :, 1 - y], y_got.at[hf], y_s.at[hf], y_r.at[hf], 1 - y, xi)

    def hop_f(hf):
        return send(f_all.at[hf, y], f_all.at[hf, y], f_s.at[hf], f_r.at[hf], 1 - y, xi)

    def turns(owner):
        row = lax.broadcasted_iota(jnp.int32, (OWN, hd), 0)
        pos = functools.reduce(lambda acc_, r: jnp.where(row == r, lens[owner * OWN + r], acc_), range(OWN), jnp.zeros((OWN, hd), jnp.int32))
        angle = pos.astype(F32) * freq[...]
        lane = lax.broadcasted_iota(jnp.int32, (OWN, hd), 1)
        return jnp.cos(angle), jnp.where(lane < hd // TWO, -jnp.sin(angle), jnp.sin(angle))

    for y_o in range(TWO):
        cos[y_o], sin[y_o] = turns(y_o * 4 + chip * TWO + core)
    for load in inputs:
        load.wait()
    h = hid[...].astype(F32).reshape(LANES, width)
    mean, rstd = norm_stats(h, stat, y, xi, st_s, st_r, ready, 4)
    normed = ((h - mean) * rstd * gain[...]).astype(BF16)
    for hf in range(TWO):
        for core_o in range(TWO):
            for chip_o in range(TWO):
                for y_o in range(TWO):
                    src = (y_o * 4 + chip_o * TWO + core_o) * OWN + hf * 8
                    dst = hf * HALF + core_o * PAIR + chip_o * OWN + y_o * 8
                    n_perm[dst:dst + 8, :] = normed[src:src + 8, :]

    for s in range(TWO):
        for i, load in enumerate(q_loads(s)):
            load.wait()
            prod = jnp.dot(n_perm[...], ring[s, i], preferred_element_type=F32)
            part_q[:, :, :, :, (TWO * s + i) * FC:(TWO * s + i + 1) * FC] = prod.reshape(TWO, TWO, TWO, OWN, FC)
        start(w_loads(RING - 3 + s))
    for load in kv_w:
        load.wait()
    part_q[..., qc:] = jnp.dot(n_perm[...], w_kv[...], preferred_element_type=F32).reshape(TWO, TWO, TWO, OWN, TWO * hd)
    hop_qa.start()

    def rotate_queries():
        hop_qb.wait_recv()
        both = part_q[:, core, chip] + ga_q[:, chip] + gb_q[...]
        total[...] = both.astype(BF16).astype(F32).reshape(TWO, TWO, 8, qc + TWO * hd)
        for y_o in range(TWO):
            cos_r, sin_r = cos[y_o], sin[y_o]
            for head in range(heads):
                val = total[:, y_o, :, head * hd:(head + 1) * hd].reshape(OWN, hd)
                q_rot[y_o, :, head * hd:(head + 1) * hd] = (val * cos_r + pltpu.roll(val, hd // TWO, 1) * sin_r).astype(BF16)
        hop_qc.start()
        key = total[:, y, :, qc:qc + hd].reshape(OWN, hd)
        value = total[:, y, :, qc + hd:].reshape(OWN, hd)
        key = (key * cos[y] + pltpu.roll(key, hd // TWO, 1) * sin[y]).astype(BF16)
        kv_out[0] = key
        kv_out[1] = value.astype(BF16)
        kn[:, 0, :] = key.astype(F32)
        vn[:, 0, :] = value
        q_full[y] = q_rot[y]

    def spread_queries():
        hop_qc.wait_recv()
        for y_o in range(TWO):
            for head in range(heads):
                q_heads[:, y_o * heads + head, :] = q_full[y_o, :, head * hd:(head + 1) * hd].astype(F32)

    def add_pair(j):
        hop_a(j).wait_recv()
        for hf in range(TWO):
            sum_at(hf, j // TWO)[j % TWO] = pool[TWO * j + hf, core, 1 - chip] + pool[TWO * steps + j, hf, 1 - chip]

        @pl.when(j % TWO == 1)
        def _():
            hop_b(0, j // TWO).start()

    def project(j, carry):
        @pl.when(j + RING - 1 < steps)
        def _():
            start(w_loads(j + RING - 1))

        slot = (j + TWO) % RING
        for i, load in enumerate(w_loads(j)):
            load.wait()
            prod = jnp.dot(n_perm[...], ring[slot, i], preferred_element_type=F32)
            pool[pl.ds(TWO * j, TWO), :, :, :, i * FC:(i + 1) * FC] = prod.reshape(TWO, TWO, TWO, OWN, FC)
        hop_a(j).start()

        @pl.when(j == 0)
        def _():
            hop_qa.wait_recv()
            sb_q[...] = part_q[:, core, 1 - chip] + ga_q[:, 1 - chip]
            hop_qb.start()

        @pl.when(j >= 1)
        def _():
            add_pair(j - 1)

        @pl.when(j == 4)
        def _():
            for b in range(KVS):
                start(cache_loads(b))

        @pl.when(j == 8)
        def _():
            rotate_queries()

        @pl.when(j == 12)
        def _():
            spread_queries()
        return carry

    lax.fori_loop(0, steps, project, 0)
    add_pair(steps - 1)
    for t in range(RING - 1):
        start(block(wd, t * WB, t))
    for i in range(4):
        tail_load(i).start()

    def activate(hf, p):
        hop_b(hf, p).wait_recv()
        for i in range(TWO):
            j = TWO * p + i
            both = pool[TWO * j + hf, core, chip] + pool[TWO * steps + j, hf, chip] + got_at(hf, p)[i]
            gate = both[:, :FC].astype(BF16).astype(F32)
            up_val = both[:, FC:].astype(BF16).astype(F32)
            cols = pl.ds(pl.multiple_of(((p % 4) * TWO + i) * FC, FC), FC)
            act[hf, p // 4, core, chip, :, cols] = (jax.nn.silu(gate) * up_val).astype(BF16)

        @pl.when(p % 4 == 3)
        def _():
            hop_m(hf, p // 4).start()

    part_len = 1024

    def attend(b):
        slot = b % KVS
        scale = hd ** -0.5
        q32 = q_heads[b]
        q = q32.astype(BF16)
        limit = lens[mine * OWN + b]
        s_new = jnp.sum(q32 * kn[b], axis=1, keepdims=True) * scale
        load_k, load_v = cache_loads(b)
        load_k.wait()
        high = None
        for i in range(length // part_len):
            rows = slice(i * part_len, (i + 1) * part_len)
            s = lax.dot_general(q, k_buf[slot, rows], (((1,), (1,)), ((), ())), preferred_element_type=F32) * scale
            pos = lax.broadcasted_iota(jnp.int32, s.shape, 1) + i * part_len
            s = jnp.where(pos < limit, s, -jnp.inf)
            scores[:, rows] = s
            for c in range(0, part_len, LANES):
                high = s[:, c:c + LANES] if high is None else jnp.maximum(high, s[:, c:c + LANES])
        best = jnp.maximum(jnp.max(high, axis=1, keepdims=True), s_new)
        mass = None
        for i in range(length // part_len):
            rows = slice(i * part_len, (i + 1) * part_len)
            e = jnp.exp(scores[:, rows] - best)
            scores[:, rows] = e
            for c in range(0, part_len, LANES):
                mass = e[:, c:c + LANES] if mass is None else mass + e[:, c:c + LANES]
        e_new = jnp.exp(s_new - best)
        inv = 1.0 / (jnp.sum(mass, axis=1, keepdims=True) + e_new)
        for i in range(length // part_len):
            rows = slice(i * part_len, (i + 1) * part_len)
            probs[:, rows] = (scores[:, rows] * inv).astype(BF16)
        load_v.wait()
        o = jnp.dot(probs[...], v_buf[slot], preferred_element_type=F32)
        o = o + (e_new * inv).astype(BF16).astype(F32) * vn[b]
        o_heads[b] = o.astype(BF16).astype(F32)

        @pl.when(b + KVS < seqs)
        def _():
            start(cache_loads(b + KVS))

    def send_heads(hf):
        for y_o in range(TWO):
            for head in range(heads):
                o_in[y_o, hf, :, head * hd:(head + 1) * hd] = o_heads[hf * 8:hf * 8 + 8, y_o * heads + head, :].astype(BF16)
        o_all[hf, core, chip, y] = o_in[y, hf]
        hop_o(hf, 0).start()

    def contract(hf):
        base = hf * (np_ + TWO * full)
        acc[hf] = jnp.zeros(acc.shape[1:], F32)

        def add(t, left):
            slot = take_item(t)
            for i in range(TWO):
                prod = jnp.dot(left, ring[slot, i], preferred_element_type=F32)
                acc[hf, :, :, :, i * hw:(i + 1) * hw] += prod.reshape(4, TWO, 8, hw)

        for g in range(TWO):
            hop_p(hf, g).wait_recv()

            def from_act(i, carry):
                add(base + g * (nd // TWO) + i, act[hf, g, :, :, :, pl.ds(pl.multiple_of(i * WB, WB), WB)].reshape(HALF, WB))
                return carry

            lax.fori_loop(0, nd // TWO, from_act, 0)
        hop_o(hf, TWO).wait_recv()

        def from_heads(i, carry):
            add(base + nd + i, o_all[hf, :, :, :, :, pl.ds(pl.multiple_of(i * WB, WB), WB)].reshape(HALF, WB))
            return carry

        lax.fori_loop(0, no, from_heads, 0)

    def finish_layer(hf, after):
        hop_y(hf).wait_recv()
        res = [hid[y * 4 + (i % TWO) * TWO + i // TWO, hf * 8:hf * 8 + 8].astype(F32) for i in range(4)]
        branch = acc[hf, :, y] + y_got[hf]
        r = jnp.concatenate(res, axis=0) + branch.reshape(PAIR, width)
        mean, rstd = norm_stats(r, stat_f.at[hf], y, xi, sf_s.at[hf], sf_r.at[hf], lambda: None, 4, after)
        f = ((r - mean) * rstd * gain_f[...]).astype(BF16)
        for i in range(4):
            f_all[hf, y, (i % TWO) * TWO + i // TWO] = f[i * 8:(i + 1) * 8]
        hop_f(hf).start()

    def each(body, low, high):
        def step(p, carry):
            body(p)
            return carry

        lax.fori_loop(low, high, step, 0)

    def pass_m(hf):
        for g in range(TWO):
            hop_m(hf, g).wait_recv()
            hop_p(hf, g).start()

    def pass_o(hf, n):
        hop_o(hf, n).wait_recv()
        hop_o(hf, n + 1).start()

    def mix(i):
        pl.when(i == 8)(lambda: send_heads(0))
        attend(i)
        pl.when(i < 8)(lambda: activate(0, i))

        @pl.when(i == 8)
        def _():
            pass_o(0, 0)
            each(lambda p: hop_b(1, p).start(), 0, HELD)

        pl.when(i == 10)(lambda: pass_m(0))
        pl.when(i == 11)(lambda: pass_o(0, 1))

        @pl.when(i == 12)
        def _():
            each(lambda j: hop_a(j).wait_send(), 0, steps)
            each(lambda p: hop_b(0, p).wait_send(), 0, 8)
            contract(0)
            hop_y(0).start()
            each(lambda p: activate(1, p), 0, TWO)

        @pl.when(i == 13)
        def _():
            finish_layer(0, lambda: each(lambda p: hop_b(1, p).start(), HELD, 8))

    each(mix, 0, seqs)
    hop_f(0).wait_recv()
    send_heads(1)
    each(lambda p: activate(1, p), TWO, 4)

    def out_at(hf, k):
        return 56 - hf * 6 + k

    def in_at(hf, k):
        return PAIR + k if hf else 20 + TWO * k

    def lhop_a(hf, k):
        return send(pool.at[k], pool.at[8 + TWO * k], la_s.at[hf, k], la_r.at[hf, k], y, partner)

    def lhop_b(hf, k):
        return send(pool.at[out_at(hf, k)], pool.at[in_at(hf, k)], lb_s.at[hf, k], lb_r.at[hf, k], y, twin)

    def lhop_c(k):
        return send(pool.at[pl.ds(6 + TWO * k, TWO)], pool.at[pl.ds(38 + TWO * k, TWO)], lc_s.at[k], lc_r.at[k], y, partner)

    def thop_a(hf):
        return send(t_a.at[hf], tg_a.at[hf], ta_s.at[hf], ta_r.at[hf], y, partner)

    def thop_b(hf):
        return send(t_b.at[hf], tg_b.at[hf], tb_s.at[hf], tb_r.at[hf], y, twin)

    thop_c = send(t_c, tg_c, tc_s.at[0], tc_r.at[0], y, partner)
    nt = (((1,), (1,)), ((), ()))

    def product(left, slot, n):
        rows = slice(n * hw, (n + 1) * hw)
        return (lax.dot_general(left[:, :hw], ring[slot, 0, rows], nt, preferred_element_type=F32)
                + lax.dot_general(left[:, hw:], ring[slot, 1, rows], nt, preferred_element_type=F32))

    def tail_product(left, i):
        return lax.dot_general(left, e_tail[i], nt, preferred_element_type=F32)

    t_a[...] = jnp.zeros_like(t_a)
    t_b[...] = jnp.zeros_like(t_b)
    t_c[...] = jnp.zeros_like(t_c)

    def outward(hf):
        def chunk(k):
            left = f_all[hf].reshape(HALF, width)
            if hf == 1:
                lhop_a(0, k).wait_send()
            slot = take_item(e_base[hf] + TWO * k)
            for n in range(TWO):
                pool[k, :, :, :, n * hw:(n + 1) * hw] = product(left, slot, n).reshape(TWO, TWO, OWN, hw)
            lhop_a(hf, k).start()
            slot = take_item(e_base[hf] + TWO * k + 1)
            for n in range(TWO):
                pool[out_at(hf, k), :, :, :, n * hw:(n + 1) * hw] = product(left, slot, n).reshape(TWO, TWO, OWN, hw)
            lhop_a(hf, k).wait_recv()
            pool[out_at(hf, k)] += pool[8 + TWO * k]
            if hf == 0:
                pl.when(k < full - TWO)(lambda: lhop_b(0, k).start())

                @pl.when(k == 0)
                def _():
                    each(lambda p: activate(1, p), 4, 8)
                    pass_o(1, 0)
            else:
                lhop_b(1, k).start()

        each(chunk, 0, full)
        left = f_all[hf].reshape(HALF, width)
        if hf == 0:
            tail_load(0).wait()
            tail_load(1).wait()
        t_a[hf, :, :rest] = tail_product(left, 0)
        thop_a(hf).start()
        t_b[hf, :, :rest] = tail_product(left, 1)
        thop_a(hf).wait_recv()
        t_b[hf] += tg_a[hf]
        if hf == 1:
            thop_b(1).start()

    def release():
        each(lambda k: lhop_b(0, k).start(), full - TWO, full)
        thop_b(0).start()

    outward(0)
    pass_m(1)
    pass_o(1, 1)
    each(lambda p: hop_b(1, p).wait_send(), 0, 8)
    contract(1)
    hop_y(1).start()
    finish_layer(1, release)
    hop_f(1).wait_recv()
    outward(1)

    for g in range(8):
        for hf in range(TWO):
            f_nat[g * OWN + hf * 8:g * OWN + hf * 8 + 8, :] = f_all[hf, g // 4, g % 4]

    def inward(k, carry):
        slot = take_item(c_base + k)
        for n in range(TWO):
            pool[pl.ds(6 + TWO * k, TWO), :, :, :, n * hw:(n + 1) * hw] = product(f_nat[...], slot, n).reshape(TWO, TWO, TWO, OWN, hw)
        lhop_c(k).start()
        return carry

    lax.fori_loop(0, full, inward, 0)
    tail_load(TWO).wait()
    t_c[:, :rest] = tail_product(f_nat[...], TWO)
    thop_c.start()
    tail_load(3).wait()

    top[...] = jnp.full_like(top, LOW)
    mass_l[...] = jnp.zeros_like(mass_l)

    def fold(z):
        tiles = [z[:, i:i + LANES] for i in range(0, z.shape[1], LANES)]
        high = functools.reduce(jnp.maximum, tiles, top[...])
        mass_l[...] = mass_l[...] * jnp.exp(top[...] - high) + sum(jnp.exp(g - high) for g in tiles)
        top[...] = high

    def weave(first, second):
        n = first.shape[-1]
        return jnp.stack([first.reshape(8, 8, n), second.reshape(8, 8, n)], axis=1).reshape(LANES, n)

    def finish(k, carry):
        slot = take_item(d_base + k)
        lhop_c(k).wait_recv()
        lhop_b(0, k).wait_recv()
        lhop_b(1, k).wait_recv()
        for n in range(TWO):
            cols = slice(n * hw, (n + 1) * hw)
            z = product(f_nat[...], slot, n) + pool[pl.ds(38 + TWO * k, TWO), :, :, :, cols].reshape(LANES, hw)
            z = z + weave(pool[in_at(0, k), :, :, :, cols], pool[in_at(1, k), :, :, :, cols])
            z_out[pl.ds(pl.multiple_of(k * WB + n * hw, hw), hw), :] = z.T
            fold(z)
        return carry

    lax.fori_loop(0, full, finish, 0)
    thop_c.wait_recv()
    thop_b(0).wait_recv()
    thop_b(1).wait_recv()
    z_tail = tg_c[...] + weave(tg_b[0], tg_b[1])
    own = tail_product(f_nat[...], 3)
    z_tail = z_tail + jnp.concatenate([own, jnp.zeros((LANES, z_tail.shape[1] - rest), F32)], axis=1)
    z_out[full * WB:, :] = z_tail.T[:rest]
    lane = lax.broadcasted_iota(jnp.int32, z_tail.shape, 1)
    fold(jnp.where(lane < rest, z_tail, LOW))

    high = jnp.max(top[...], axis=1, keepdims=True)
    stat_z[mine] = to_lanes(high, jnp.sum(mass_l[...] * jnp.exp(top[...] - high), axis=1, keepdims=True))
    copies = []
    for dy in range(TWO):
        for d in range(4):
            if dy or d:
                i = dy * 4 + d - 1
                copies.append(send(stat_z.at[mine], stat_z.at[mine], sz_s.at[i], sz_r.at[i],
                                   y + dy * (1 - TWO * y), (xi + d) % 4))
    start(copies)
    for copy in copies:
        copy.wait()
    highs = [stat_z[i][0:1] for i in range(8)]
    best_all = functools.reduce(jnp.maximum, highs)
    lse_out[...] = best_all + jnp.log(sum(stat_z[i][1:TWO] * jnp.exp(highs[i] - best_all) for i in range(8)))

    def drain_logits(k, carry):
        lhop_a(1, k).wait_send()
        lhop_b(0, k).wait_send()
        lhop_b(1, k).wait_send()
        lhop_c(k).wait_send()
        return carry

    lax.fori_loop(0, full, drain_logits, 0)
    for hf in range(TWO):
        for g in range(TWO):
            hop_m(hf, g).wait_send()
            hop_p(hf, g).wait_send()
        for n in range(3):
            hop_o(hf, n).wait_send()
        for hop in (hop_y, hop_f, thop_a, thop_b):
            hop(hf).wait_send()
    for hop in (hop_qa, hop_qb, hop_qc, thop_c):
        hop.wait_send()


def step_call(lens, hid, gain, gain_f, freq, wq, wk, wv, wg, wu, wo, wd, emb, k_cache, v_cache):
    width = hid.shape[TWO]
    qc, hd = wq.shape[1], wk.shape[1]
    seqs, length, _ = k_cache.shape
    cols = qc + TWO * hd
    steps = wg.shape[1] // FC
    heads = TWO * qc // hd
    share = emb.shape[0] // QUAD
    full = share // WB
    rest = share - full * WB
    tail_w = -(-rest // LANES) * LANES
    vmem = pl.BlockSpec(memory_space=pltpu.VMEM)
    hbm = pl.BlockSpec(memory_space=pl.ANY)

    def f32(*shape):
        return pltpu.VMEM(shape, F32)

    def bf16(*shape):
        return pltpu.VMEM(shape, BF16)

    def dma(*shape):
        return pltpu.SemaphoreType.DMA(shape)

    return pl.pallas_call(
        step_kernel, name="step",
        out_shape=[jax.ShapeDtypeStruct((TWO, OWN, hd), BF16), jax.ShapeDtypeStruct((share, LANES), F32),
                   jax.ShapeDtypeStruct((1, LANES), F32)],
        in_specs=[pl.BlockSpec(memory_space=pltpu.SMEM)] + [hbm] * 3 + [vmem] + [hbm] * 10, out_specs=[vmem] * 3,
        scratch_shapes=[
            bf16(OCT, OWN, width), f32(1, width), f32(1, width), f32(TWO, OWN, hd), f32(TWO, OWN, hd),
            bf16(LANES, width), bf16(RING, TWO, width, FC), bf16(width, TWO * hd),
            f32(TWO, TWO, TWO, OWN, cols), f32(TWO, TWO, OWN, cols), f32(TWO, OWN, cols), f32(TWO, OWN, cols), f32(TWO, TWO, OCT, cols),
            bf16(TWO, OWN, qc), bf16(TWO, OWN, qc), f32(seqs, heads, hd), f32(seqs, heads, hd), f32(seqs, 1, hd), f32(seqs, 1, hd),
            f32(QUAD * steps, TWO, TWO, OWN, TWO * FC), bf16(TWO, TWO, TWO, TWO, OWN, steps // TWO * FC),
            bf16(TWO, TWO, OCT, qc), bf16(TWO, TWO, TWO, TWO, OCT, qc),
            bf16(KVS, length, hd), bf16(KVS, length, hd), f32(heads, length), bf16(heads, length),
            f32(TWO, QUAD, TWO, OCT, width), f32(TWO, QUAD, OCT, width), bf16(TWO, TWO, QUAD, OCT, width), bf16(LANES, width), bf16(QUAD, rest, width),
            f32(TWO, HALF, tail_w), f32(TWO, HALF, tail_w), f32(TWO, HALF, tail_w), f32(TWO, HALF, tail_w), f32(LANES, tail_w), f32(LANES, tail_w),
            f32(LANES, LANES), f32(LANES, LANES), f32(QUAD, OCT, LANES), f32(TWO, QUAD, OCT, LANES), f32(OCT, OCT, LANES),
            dma(3), dma(RING, TWO), dma(TWO), dma(QUAD), dma(KVS), dma(KVS), dma(steps), dma(steps), dma(TWO, steps // TWO), dma(TWO, steps // TWO),
            dma(TWO, TWO), dma(TWO, TWO), dma(TWO, TWO), dma(TWO, TWO), dma(3), dma(3),
            dma(TWO, 3), dma(TWO, 3), dma(TWO), dma(TWO), dma(TWO), dma(TWO), dma(3), dma(3), dma(TWO, 3), dma(TWO, 3),
            dma(TWO, full), dma(TWO, full), dma(TWO, full), dma(TWO, full), dma(full), dma(full),
            dma(TWO), dma(TWO), dma(TWO), dma(TWO), dma(1), dma(1), dma(7), dma(7)],
        compiler_params=pltpu.CompilerParams(collective_id=0, has_side_effects=True, vmem_limit_bytes=63 * TWO**20),
    )(lens, hid, gain, gain_f, freq, wq, wk, wv, wg, wu, wo, wd, emb, k_cache, v_cache)


def solution(mesh):
    row_spec = P(("dp", "yax", "xax"))

    def local_step(hidden, cache_len, k_cache, v_cache, g_attn, w_query, w_key, w_value,
                   w_gate, w_up, w_out, w_down, g_final, embedding):
        width = hidden.shape[1]
        own_rows, _, head_dim = k_cache.shape
        half = head_dim // TWO
        lane = jnp.arange(head_dim)
        inv_freq = ROPE_BASE ** (-((lane % half).astype(F32) * 2.0) / head_dim)
        kv_new, logits_t, log_norm = step_call(
            cache_len, hidden.reshape(8, own_rows, width), g_attn[None], g_final[None], inv_freq[None],
            w_query, w_key, w_value, w_gate, w_up, w_out, w_down, embedding, k_cache, v_cache)
        return kv_new[0], kv_new[1], (logits_t - log_norm).T, log_norm[0]

    in_specs = (P("dp", "xax"), P("dp"), row_spec, row_spec, P("xax"), P("xax", "yax"),
                P("xax", None), P("xax", None), P("xax", "yax"), P("xax", "yax"),
                P("yax", "xax"), P("yax", "xax"), P("xax"), P("yax", "xax"))
    out_specs = (row_spec, row_spec, P("dp", ("yax", "xax")), P("dp"))
    return jax.shard_map(local_step, mesh=mesh, in_specs=in_specs, out_specs=out_specs, check_vma=False)
```

time: 513 us -> 167 us (0.33)
  blocking collectives: 237 us -> 0 us
  Pallas kernels: 0 us -> 160 us
  waiting for transfers between devices: 124 us -> 0 us
  matrix products: 103 us -> 0 us
  other arithmetic: 24.6 us -> 4.34 us
  between operations: 14.3 us -> 0.65 us
  starting transfers between devices: 7.24 us -> 0 us
    psum x4 -> x0, blocking collectives: 205 us -> none  [the longest x1 166 us: local_step(): projected = lax.psum(proj_part, 'xax').astype(jnp.bfloat16)]
    pallas_call x0 -> x1, Pallas kernels: none -> 160 us  [step_call(): pl.pallas_call(step_kernel, name='step', out_shape=[jax.ShapeDtypeStruct(...]
    dot_general x11 -> x0, matrix products: 103 us -> none  [the longest x1 24.6 us: local_step(): jnp.einsum('bd,vd->bv', final_norm, embedding, preferred_element_type=jnp...]
    reduce_scatter x1 -> x0, waiting for transfers between devices: 92.3 us -> none  [local_step(): lax.psum_scatter(logit_part, 'xax', scatter_dimension=1, tiled=True)]
    psum x1 -> x0, waiting for transfers between devices: 23.8 us -> none  [local_step(): residual_out = residual + lax.psum(branch_sum, 'yax')]
    pmax x1 -> x0, blocking collectives: 22.2 us -> none  [local_step(): row_max = lax.pmax(jnp.max(logits, axis=1), ('yax', 'xax'))]
    reduce_sum x4 -> x0, other arithmetic: 13.3 us -> none  [the longest x1 8.18 us: attend_local(): denominator = jnp.sum(weights, axis=-1) + weight_new]
    all_gather x1 -> x0, blocking collectives: 9.66 us -> none  [local_step(): attn_grp = lax.all_gather(attn_own, 'xax', axis=0, tiled=True)]
  transfers between devices with their start and end apart: 4 -> 0, of which waited for: 3 -> 0; matrix products, arithmetic and copies ran while one was open for 2% -> 0% of each run, Pallas kernels for 0% -> 0%
where the time goes in v3:
time: 167 us; the launch traced here: 166 us
  Pallas kernels  160 us (96%)
  other arithmetic  4.34 us (3%)
  local copies, waits for them, and re-layouts  1.8 us (1%)
    pallas_call x1, Pallas kernels, step_call(): pl.pallas_call(step_kernel, name='step', out_shape=[jax.ShapeDtypeStruct(...  160 us
    transpose x1, other arithmetic, local_step(): return (kv_new[0], kv_new[1], (logits_t - log_norm).T, log_norm[0])  3.81 us

profile of v3, /device:TPU:0, one launch (start us, length us, event | category | flops | bytes accessed | tf_op | source)
XLA Modules:
  0.0 166.4 jit_solution(14660183730539607144)
XLA Ops:
  0.6 0.5 fusion.4.freq
  1.2 159.6 %step.1 = (bf16[2,16,128]{2,1,0:T(8,128)(2,1)}, f32[6304,128]{1,0:T(8,128)}, f32[1,128]{1,0:T(1,128)}) custom-call(s32[128]{0:T(128)} %lens.1, bf16[8,16,1024]{2,1,0:T(8,128)(2,1)} %bitcast.10, f32[1,1024]{1,0:T(1,128)} %bitcast.11, f32[1,1024]{1,0:T(1,128)} %bitcast.12, f32[1,128]{1,0:T(1,128)} %fusion.4.freq, bf16[1024,2048]{1,0:T(8,128)(2,1)} %wq.1, ...), custom_call_target="tpu_custom_call" | custom-call | tf_op jit(solution)/shard_map/step/pallas_call | solution.py:672
  160.7 0.0 copy-start
  160.8 1.3 slice_bitcast_fusion
  162.0 3.8 %subtract_bitcast_fusion = f32[128,6304]{0,1:T(8,128)} fusion(f32[6304,128]{1,0:T(8,128)} %get-tuple-element.8, f32[128]{0:T(128)} %bitcast.13), kind=kLoop, calls=%fused_computation | loop fusion | flops 806912 | bytes 6455808 | tf_op jit(solution)/shard_map/transpose | solution.py:710
  165.9 0.0 copy-done
  165.9 0.5 copy.19
Async XLA Ops:
  160.7 5.1 %copy-start = (f32[1,128]{1,0:T(1,128)S(1)}, f32[1,128]{1,0:T(1,128)}, u32[]{:S(2)}) copy-start(f32[1,128]{1,0:T(1,128)} %get-tuple-element.9) | copy-start | bytes 1540

commit v4 on v3

--- a/solution.py
+++ b/solution.py
@@ -75,15 +75,15 @@
 WB = 1024
 RING = 6
 KVS = 3
-HELD = 5
+HELD = 6
 
 
 def step_kernel(lens, hid_h, gain_h, gain_fh, freq, wq, wk, wv, wg, wu, wo, wd, emb, k_hbm, v_hbm,
-                kv_out, z_out, lse_out,
+                kv_out, z_out, lse_out, kv_v, z_v,
                 hid, gain, gain_f, cos, sin, n_perm, ring, w_kv, part_q, ga_q, sb_q, gb_q, total, q_rot, q_full, q_heads, o_heads, kn, vn,
                 pool, act, o_in, o_all, k_buf, v_buf, scores, probs, acc, y_got, f_all, f_nat, e_tail,
                 t_a, t_b, tg_a, tg_b, t_c, tg_c, top, mass_l, stat, stat_f, stat_z,
-                i_sem, r_sem, kv_sem, tail_sem, k_sem, v_sem, a_s, a_r, b_s, b_r, m_s, m_r, p_s, p_r, q_s, q_r,
+                i_sem, z_sem, r_sem, kv_sem, tail_sem, k_sem, v_sem, a_s, a_r, b_s, b_r, m_s, m_r, p_s, p_r, q_s, q_r,
                 o_s, o_r, y_s, y_r, f_s, f_r, st_s, st_r, sf_s, sf_r,
                 la_s, la_r, lb_s, lb_r, lc_s, lc_r, ta_s, ta_r, tb_s, tb_r, tc_s, tc_r, sz_s, sz_r):
     y, xi, chip, core, partner, twin = place()
@@ -220,8 +220,6 @@
         lane = lax.broadcasted_iota(jnp.int32, (OWN, hd), 1)
         return jnp.cos(angle), jnp.where(lane < hd // TWO, -jnp.sin(angle), jnp.sin(angle))
 
-    for y_o in range(TWO):
-        cos[y_o], sin[y_o] = turns(y_o * 4 + chip * TWO + core)
     for load in inputs:
         load.wait()
     h = hid[...].astype(F32).reshape(LANES, width)
@@ -245,6 +243,12 @@
         load.wait()
     part_q[..., qc:] = jnp.dot(n_perm[...], w_kv[...], preferred_element_type=F32).reshape(TWO, TWO, TWO, OWN, TWO * hd)
     hop_qa.start()
+
+    kv_store = pltpu.make_async_copy(kv_v, kv_out, z_sem.at[full + 1])
+
+    def z_store(k, size):
+        rows = pl.ds(pl.multiple_of(k * WB, 8), size)
+        return pltpu.make_async_copy(z_v.at[rows], z_out.at[rows], z_sem.at[k])
 
     def rotate_queries():
         hop_qb.wait_recv()
@@ -259,8 +263,9 @@
         key = total[:, y, :, qc:qc + hd].reshape(OWN, hd)
         value = total[:, y, :, qc + hd:].reshape(OWN, hd)
         key = (key * cos[y] + pltpu.roll(key, hd // TWO, 1) * sin[y]).astype(BF16)
-        kv_out[0] = key
-        kv_out[1] = value.astype(BF16)
+        kv_v[0] = key
+        kv_v[1] = value.astype(BF16)
+        kv_store.start()
         kn[:, 0, :] = key.astype(F32)
         vn[:, 0, :] = value
         q_full[y] = q_rot[y]
@@ -301,6 +306,10 @@
         @pl.when(j >= 1)
         def _():
             add_pair(j - 1)
+
+        @pl.when((j == TWO) | (j == 3))
+        def _():
+            cos[j - TWO], sin[j - TWO] = turns((j - TWO) * 4 + chip * TWO + core)
 
         @pl.when(j == 4)
         def _():
@@ -586,29 +595,33 @@
         n = first.shape[-1]
         return jnp.stack([first.reshape(8, 8, n), second.reshape(8, 8, n)], axis=1).reshape(LANES, n)
 
-    def finish(k, carry):
+    def finish(k):
         slot = take_item(d_base + k)
         lhop_c(k).wait_recv()
+        here = pl.ds(38 + TWO * k, TWO)
+        for n in range(TWO):
+            cols = slice(n * hw, (n + 1) * hw)
+            pool[here, :, :, :, cols] += product(f_nat[...], slot, n).reshape(TWO, TWO, TWO, OWN, hw)
         lhop_b(0, k).wait_recv()
         lhop_b(1, k).wait_recv()
         for n in range(TWO):
             cols = slice(n * hw, (n + 1) * hw)
-            z = product(f_nat[...], slot, n) + pool[pl.ds(38 + TWO * k, TWO), :, :, :, cols].reshape(LANES, hw)
+            z = pool[here, :, :, :, cols].reshape(LANES, hw)
             z = z + weave(pool[in_at(0, k), :, :, :, cols], pool[in_at(1, k), :, :, :, cols])
-            z_out[pl.ds(pl.multiple_of(k * WB + n * hw, hw), hw), :] = z.T
+            z_v[pl.ds(pl.multiple_of(k * WB + n * hw, hw), hw), :] = z.T
             fold(z)
-        return carry
-
-    lax.fori_loop(0, full, finish, 0)
+        z_store(k, WB).start()
+
     thop_c.wait_recv()
+    tg_c[:, :rest] += tail_product(f_nat[...], 3)
+    each(finish, 0, full)
     thop_b(0).wait_recv()
     thop_b(1).wait_recv()
     z_tail = tg_c[...] + weave(tg_b[0], tg_b[1])
-    own = tail_product(f_nat[...], 3)
-    z_tail = z_tail + jnp.concatenate([own, jnp.zeros((LANES, z_tail.shape[1] - rest), F32)], axis=1)
-    z_out[full * WB:, :] = z_tail.T[:rest]
     lane = lax.broadcasted_iota(jnp.int32, z_tail.shape, 1)
     fold(jnp.where(lane < rest, z_tail, LOW))
+    z_v[full * WB:, :] = z_tail.T[:rest]
+    z_store(full, rest).start()
 
     high = jnp.max(top[...], axis=1, keepdims=True)
     stat_z[mine] = to_lanes(high, jnp.sum(mass_l[...] * jnp.exp(top[...] - high), axis=1, keepdims=True))
@@ -626,6 +639,9 @@
     best_all = functools.reduce(jnp.maximum, highs)
     lse_out[...] = best_all + jnp.log(sum(stat_z[i][1:TWO] * jnp.exp(highs[i] - best_all) for i in range(8)))
 
+    each(lambda k: z_store(k, WB).wait(), 0, full)
+    z_store(full, rest).wait()
+    kv_store.wait()
     def drain_logits(k, carry):
         lhop_a(1, k).wait_send()
         lhop_b(0, k).wait_send()
@@ -673,9 +689,9 @@
         step_kernel, name="step",
         out_shape=[jax.ShapeDtypeStruct((TWO, OWN, hd), BF16), jax.ShapeDtypeStruct((share, LANES), F32),
                    jax.ShapeDtypeStruct((1, LANES), F32)],
-        in_specs=[pl.BlockSpec(memory_space=pltpu.SMEM)] + [hbm] * 3 + [vmem] + [hbm] * 10, out_specs=[vmem] * 3,
+        in_specs=[pl.BlockSpec(memory_space=pltpu.SMEM)] + [hbm] * 3 + [vmem] + [hbm] * 10, out_specs=[hbm, hbm, vmem],
         scratch_shapes=[
-            bf16(OCT, OWN, width), f32(1, width), f32(1, width), f32(TWO, OWN, hd), f32(TWO, OWN, hd),
+            bf16(TWO, OWN, hd), f32(share, LANES), bf16(OCT, OWN, width), f32(1, width), f32(1, width), f32(TWO, OWN, hd), f32(TWO, OWN, hd),
             bf16(LANES, width), bf16(RING, TWO, width, FC), bf16(width, TWO * hd),
             f32(TWO, TWO, TWO, OWN, cols), f32(TWO, TWO, OWN, cols), f32(TWO, OWN, cols), f32(TWO, OWN, cols), f32(TWO, TWO, OCT, cols),
             bf16(TWO, OWN, qc), bf16(TWO, OWN, qc), f32(seqs, heads, hd), f32(seqs, heads, hd), f32(seqs, 1, hd), f32(seqs, 1, hd),
@@ -685,13 +701,47 @@
             f32(TWO, QUAD, TWO, OCT, width), f32(TWO, QUAD, OCT, width), bf16(TWO, TWO, QUAD, OCT, width), bf16(LANES, width), bf16(QUAD, rest, width),
             f32(TWO, HALF, tail_w), f32(TWO, HALF, tail_w), f32(TWO, HALF, tail_w), f32(TWO, HALF, tail_w), f32(LANES, tail_w), f32(LANES, tail_w),
             f32(LANES, LANES), f32(LANES, LANES), f32(QUAD, OCT, LANES), f32(TWO, QUAD, OCT, LANES), f32(OCT, OCT, LANES),
-            dma(3), dma(RING, TWO), dma(TWO), dma(QUAD), dma(KVS), dma(KVS), dma(steps), dma(steps), dma(TWO, steps // TWO), dma(TWO, steps // TWO),
+            dma(3), dma(full + TWO), dma(RING, TWO), dma(TWO), dma(QUAD), dma(KVS), dma(KVS), dma(steps), dma(steps), dma(TWO, steps // TWO), dma(TWO, steps // TWO),
             dma(TWO, TWO), dma(TWO, TWO), dma(TWO, TWO), dma(TWO, TWO), dma(3), dma(3),
             dma(TWO, 3), dma(TWO, 3), dma(TWO), dma(TWO), dma(TWO), dma(TWO), dma(3), dma(3), dma(TWO, 3), dma(TWO, 3),
             dma(TWO, full), dma(TWO, full), dma(TWO, full), dma(TWO, full), dma(full), dma(full),
             dma(TWO), dma(TWO), dma(TWO), dma(TWO), dma(1), dma(1), dma(7), dma(7)],
         compiler_params=pltpu.CompilerParams(collective_id=0, has_side_effects=True, vmem_limit_bytes=63 * TWO**20),
     )(lens, hid, gain, gain_f, freq, wq, wk, wv, wg, wu, wo, wd, emb, k_cache, v_cache)
+
+
+def close_kernel(z_in, lse, kv, out, k_out, v_out, lse_out, buf, in_sem, out_sem):
+    parts = buf.shape[0]
+    rows = buf.shape[1]
+    loads = [pltpu.make_async_copy(z_in.at[pl.ds(i * rows, rows)], buf.at[i], in_sem.at[i]) for i in range(parts)]
+    stores = [pltpu.make_async_copy(buf.at[i], out.at[pl.ds(i * rows, rows)], out_sem.at[i]) for i in range(parts)]
+    for load in loads:
+        load.start()
+    k_out[...] = kv[0]
+    v_out[...] = kv[1]
+    lse_out[...] = lse[...]
+    for i in range(parts):
+        loads[i].wait()
+        buf[i] = buf[i] - lse[...]
+        stores[i].start()
+    for store in stores:
+        store.wait()
+
+
+def close_call(z, lse, kv):
+    share, rows = z.shape
+    parts = 4
+    vmem = pl.BlockSpec(memory_space=pltpu.VMEM)
+    hbm = pl.BlockSpec(memory_space=pl.ANY)
+    small = jax.ShapeDtypeStruct(kv.shape[1:], BF16)
+    return pl.pallas_call(
+        close_kernel, name="close",
+        out_shape=[jax.ShapeDtypeStruct((share, rows), F32), small, small, jax.ShapeDtypeStruct((1, rows), F32)],
+        in_specs=[hbm, vmem, vmem], out_specs=[hbm, vmem, vmem, vmem],
+        scratch_shapes=[pltpu.VMEM((parts, share // parts, rows), F32),
+                        pltpu.SemaphoreType.DMA((parts,)), pltpu.SemaphoreType.DMA((parts,))],
+        compiler_params=pltpu.CompilerParams(vmem_limit_bytes=63 * 2**20),
+    )(z, lse, kv)
 
 
 def solution(mesh):
@@ -707,7 +757,8 @@
         kv_new, logits_t, log_norm = step_call(
             cache_len, hidden.reshape(8, own_rows, width), g_attn[None], g_final[None], inv_freq[None],
             w_query, w_key, w_value, w_gate, w_up, w_out, w_down, embedding, k_cache, v_cache)
-        return kv_new[0], kv_new[1], (logits_t - log_norm).T, log_norm[0]
+        log_probs, key_own, value_own, log_norm = close_call(logits_t, log_norm, kv_new)
+        return key_own, value_own, log_probs.T, log_norm[0]
 
     in_specs = (P("dp", "xax"), P("dp"), row_spec, row_spec, P("xax"), P("xax", "yax"),
                 P("xax", None), P("xax", None), P("xax", "yax"), P("xax", "yax"),

time: 167 us -> 164 us (0.982)
  other arithmetic: 4.34 us -> 0.52 us
  Pallas kernels: 160 us -> 162 us
  local copies, waits for them, and re-layouts: 1.8 us -> 0 us
    pallas_call x0 -> x1, Pallas kernels: none -> 4.25 us  [close_call(): pl.pallas_call(close_kernel, name='close', out_shape=[jax.ShapeDtypeStruc...]
    transpose x1 -> x0, other arithmetic: 3.81 us -> none  [local_step(): return (kv_new[0], kv_new[1], (logits_t - log_norm).T, log_norm[0])]
where the time goes in v4:
time: 164 us
  Pallas kernels  162 us (99%)
    pallas_call x1, Pallas kernels, step_call(): pl.pallas_call(step_kernel, name='step', out_shape=[jax.ShapeDtypeStruct(...  158 us
    pallas_call x1, Pallas kernels, close_call(): pl.pallas_call(close_kernel, name='close', out_shape=[jax.ShapeDtypeStruc...  4.25 us

profile of v4, /device:TPU:0, one launch (start us, length us, event | category | flops | bytes accessed | tf_op | source)
XLA Modules:
  0.0 163.6 jit_solution(13903994644214536005)
XLA Ops:
  0.6 0.5 fusion.4.freq
  1.2 158.2 %step.1 = (bf16[2,16,128]{2,1,0:T(8,128)(2,1)}, f32[6304,128]{1,0:T(8,128)}, f32[1,128]{1,0:T(1,128)}) custom-call(s32[128]{0:T(128)} %lens.1, bf16[8,16,1024]{2,1,0:T(8,128)(2,1)} %bitcast.5, f32[1,1024]{1,0:T(1,128)} %bitcast.6, f32[1,1024]{1,0:T(1,128)} %bitcast.7, f32[1,128]{1,0:T(1,128)} %fusion.4.freq, bf16[1024,2048]{1,0:T(8,128)(2,1)} %wq.1, ...), custom_call_target="tpu_custom_call" | custom-call | tf_op jit(solution)/shard_map/step/pallas_call | solution.py:688
  159.4 4.2 %close.1 = (f32[6304,128]{1,0:T(8,128)}, bf16[16,128]{1,0:T(8,128)(2,1)}, bf16[16,128]{1,0:T(8,128)(2,1)}, f32[1,128]{1,0:T(1,128)}) custom-call(f32[6304,128]{1,0:T(8,128)} %get-tuple-element.11.z_in, f32[1,128]{1,0:T(1,128)} %get-tuple-element.12.lse, bf16[2,16,128]{2,1,0:T(8,128)(2,1)} %get-tuple-element.13.kv), custom_call_target="tpu_custom_call" | custom-call | tf_op jit(solution)/shard_map/close/pallas_call | solution.py:737

commit v5 on v4

--- a/solution.py
+++ b/solution.py
@@ -75,15 +75,16 @@
 WB = 1024
 RING = 6
 KVS = 3
+VLIM = 121 * 2**19
 HELD = 6
 
 
 def step_kernel(lens, hid_h, gain_h, gain_fh, freq, wq, wk, wv, wg, wu, wo, wd, emb, k_hbm, v_hbm,
-                kv_out, z_out, lse_out, kv_v, z_v,
+                kv_out, z_out, lse_out,
                 hid, gain, gain_f, cos, sin, n_perm, ring, w_kv, part_q, ga_q, sb_q, gb_q, total, q_rot, q_full, q_heads, o_heads, kn, vn,
                 pool, act, o_in, o_all, k_buf, v_buf, scores, probs, acc, y_got, f_all, f_nat, e_tail,
                 t_a, t_b, tg_a, tg_b, t_c, tg_c, top, mass_l, stat, stat_f, stat_z,
-                i_sem, z_sem, r_sem, kv_sem, tail_sem, k_sem, v_sem, a_s, a_r, b_s, b_r, m_s, m_r, p_s, p_r, q_s, q_r,
+                i_sem, r_sem, kv_sem, tail_sem, k_sem, v_sem, a_s, a_r, b_s, b_r, m_s, m_r, p_s, p_r, q_s, q_r,
                 o_s, o_r, y_s, y_r, f_s, f_r, st_s, st_r, sf_s, sf_r,
                 la_s, la_r, lb_s, lb_r, lc_s, lc_r, ta_s, ta_r, tb_s, tb_r, tc_s, tc_r, sz_s, sz_r):
     y, xi, chip, core, partner, twin = place()
@@ -104,6 +105,10 @@
         for copy in copies:
             copy.start()
 
+    inputs = [pltpu.make_async_copy(src, dst, i_sem.at[i])
+              for i, (src, dst) in enumerate(((hid_h, hid), (gain_h, gain), (gain_fh, gain_f)))]
+    start(inputs)
+
     def q_loads(s):
         return [pltpu.make_async_copy(wq.at[:, pl.ds((TWO * s + i) * FC, FC)], ring.at[s, i], r_sem.at[s, i]) for i in range(TWO)]
 
@@ -112,9 +117,6 @@
         slot = (j + TWO) % RING
         return [pltpu.make_async_copy(w.at[:, cols], ring.at[slot, i], r_sem.at[slot, i]) for i, w in enumerate((wg, wu))]
 
-    inputs = [pltpu.make_async_copy(src, dst, i_sem.at[i])
-              for i, (src, dst) in enumerate(((hid_h, hid), (gain_h, gain), (gain_fh, gain_f)))]
-    start(inputs)
     kv_w = [pltpu.make_async_copy(w, w_kv.at[:, pl.ds(i * hd, hd)], kv_sem.at[i]) for i, w in enumerate((wk, wv))]
     start(q_loads(0))
     start(q_loads(1))
@@ -196,9 +198,17 @@
     def hop_p(hf, g):
         return send(act.at[hf, g, core], act.at[hf, g, core], p_s.at[hf, g], p_r.at[hf, g], y, partner)
 
-    hop_qa = send(part_q.at[:, 1 - core], ga_q, q_s.at[0], q_r.at[0], y, partner)
-    hop_qb = send(sb_q, gb_q, q_s.at[1], q_r.at[1], y, twin)
-    hop_qc = send(q_rot.at[1 - y], q_full.at[y], q_s.at[TWO], q_r.at[TWO], 1 - y, xi)
+    q_cols = (pl.ds(0, TWO * FC), pl.ds(TWO * FC, qc + TWO * hd - TWO * FC))
+    hop_qa = [send(part_q.at[:, 1 - core, :, :, cut], ga_q.at[..., cut], q_s.at[i, 0], q_r.at[i, 0], y, partner)
+              for i, cut in enumerate(q_cols)]
+    hop_qb = [send(sb_q.at[..., cut], gb_q.at[..., cut], q_s.at[i, 1], q_r.at[i, 1], y, twin) for i, cut in enumerate(q_cols)]
+
+    def pair_queries(i):
+        hop_qa[i].wait_recv()
+        sb_q[:, :, q_cols[i]] = part_q[:, core, 1 - chip, :, q_cols[i]] + ga_q[:, 1 - chip, :, q_cols[i]]
+        hop_qb[i].start()
+
+    hop_qc = send(q_rot.at[1 - y], q_full.at[y], q_s.at[0, TWO], q_r.at[0, TWO], 1 - y, xi)
 
     def hop_o(hf, n):
         if n == 0:
@@ -239,19 +249,17 @@
             prod = jnp.dot(n_perm[...], ring[s, i], preferred_element_type=F32)
             part_q[:, :, :, :, (TWO * s + i) * FC:(TWO * s + i + 1) * FC] = prod.reshape(TWO, TWO, TWO, OWN, FC)
         start(w_loads(RING - 3 + s))
+        if s == 0:
+            hop_qa[0].start()
     for load in kv_w:
         load.wait()
     part_q[..., qc:] = jnp.dot(n_perm[...], w_kv[...], preferred_element_type=F32).reshape(TWO, TWO, TWO, OWN, TWO * hd)
-    hop_qa.start()
-
-    kv_store = pltpu.make_async_copy(kv_v, kv_out, z_sem.at[full + 1])
-
-    def z_store(k, size):
-        rows = pl.ds(pl.multiple_of(k * WB, 8), size)
-        return pltpu.make_async_copy(z_v.at[rows], z_out.at[rows], z_sem.at[k])
+    hop_qa[1].start()
+    pair_queries(0)
 
     def rotate_queries():
-        hop_qb.wait_recv()
+        hop_qb[0].wait_recv()
+        hop_qb[1].wait_recv()
         both = part_q[:, core, chip] + ga_q[:, chip] + gb_q[...]
         total[...] = both.astype(BF16).astype(F32).reshape(TWO, TWO, 8, qc + TWO * hd)
         for y_o in range(TWO):
@@ -263,9 +271,8 @@
         key = total[:, y, :, qc:qc + hd].reshape(OWN, hd)
         value = total[:, y, :, qc + hd:].reshape(OWN, hd)
         key = (key * cos[y] + pltpu.roll(key, hd // TWO, 1) * sin[y]).astype(BF16)
-        kv_v[0] = key
-        kv_v[1] = value.astype(BF16)
-        kv_store.start()
+        kv_out[0] = key
+        kv_out[1] = value.astype(BF16)
         kn[:, 0, :] = key.astype(F32)
         vn[:, 0, :] = value
         q_full[y] = q_rot[y]
@@ -299,9 +306,7 @@
 
         @pl.when(j == 0)
         def _():
-            hop_qa.wait_recv()
-            sb_q[...] = part_q[:, core, 1 - chip] + ga_q[:, 1 - chip]
-            hop_qb.start()
+            pair_queries(1)
 
         @pl.when(j >= 1)
         def _():
@@ -608,9 +613,8 @@
             cols = slice(n * hw, (n + 1) * hw)
             z = pool[here, :, :, :, cols].reshape(LANES, hw)
             z = z + weave(pool[in_at(0, k), :, :, :, cols], pool[in_at(1, k), :, :, :, cols])
-            z_v[pl.ds(pl.multiple_of(k * WB + n * hw, hw), hw), :] = z.T
+            z_out[pl.ds(pl.multiple_of(k * WB + n * hw, hw), hw), :] = z.T
             fold(z)
-        z_store(k, WB).start()
 
     thop_c.wait_recv()
     tg_c[:, :rest] += tail_product(f_nat[...], 3)
@@ -620,8 +624,7 @@
     z_tail = tg_c[...] + weave(tg_b[0], tg_b[1])
     lane = lax.broadcasted_iota(jnp.int32, z_tail.shape, 1)
     fold(jnp.where(lane < rest, z_tail, LOW))
-    z_v[full * WB:, :] = z_tail.T[:rest]
-    z_store(full, rest).start()
+    z_out[full * WB:, :] = z_tail.T[:rest]
 
     high = jnp.max(top[...], axis=1, keepdims=True)
     stat_z[mine] = to_lanes(high, jnp.sum(mass_l[...] * jnp.exp(top[...] - high), axis=1, keepdims=True))
@@ -639,9 +642,6 @@
     best_all = functools.reduce(jnp.maximum, highs)
     lse_out[...] = best_all + jnp.log(sum(stat_z[i][1:TWO] * jnp.exp(highs[i] - best_all) for i in range(8)))
 
-    each(lambda k: z_store(k, WB).wait(), 0, full)
-    z_store(full, rest).wait()
-    kv_store.wait()
     def drain_logits(k, carry):
         lhop_a(1, k).wait_send()
         lhop_b(0, k).wait_send()
@@ -658,7 +658,7 @@
             hop_o(hf, n).wait_send()
         for hop in (hop_y, hop_f, thop_a, thop_b):
             hop(hf).wait_send()
-    for hop in (hop_qa, hop_qb, hop_qc, thop_c):
+    for hop in (*hop_qa, *hop_qb, hop_qc, thop_c):
         hop.wait_send()
 
 
@@ -687,11 +687,10 @@
 
     return pl.pallas_call(
         step_kernel, name="step",
-        out_shape=[jax.ShapeDtypeStruct((TWO, OWN, hd), BF16), jax.ShapeDtypeStruct((share, LANES), F32),
-                   jax.ShapeDtypeStruct((1, LANES), F32)],
-        in_specs=[pl.BlockSpec(memory_space=pltpu.SMEM)] + [hbm] * 3 + [vmem] + [hbm] * 10, out_specs=[hbm, hbm, vmem],
+        out_shape=[bf16(TWO, OWN, hd), f32(share, LANES), f32(1, LANES)],
+        in_specs=[pl.BlockSpec(memory_space=pltpu.SMEM)] + [hbm] * 3 + [vmem] + [hbm] * 10, out_specs=[vmem] * 3,
         scratch_shapes=[
-            bf16(TWO, OWN, hd), f32(share, LANES), bf16(OCT, OWN, width), f32(1, width), f32(1, width), f32(TWO, OWN, hd), f32(TWO, OWN, hd),
+            bf16(OCT, OWN, width), f32(1, width), f32(1, width), f32(TWO, OWN, hd), f32(TWO, OWN, hd),
             bf16(LANES, width), bf16(RING, TWO, width, FC), bf16(width, TWO * hd),
             f32(TWO, TWO, TWO, OWN, cols), f32(TWO, TWO, OWN, cols), f32(TWO, OWN, cols), f32(TWO, OWN, cols), f32(TWO, TWO, OCT, cols),
             bf16(TWO, OWN, qc), bf16(TWO, OWN, qc), f32(seqs, heads, hd), f32(seqs, heads, hd), f32(seqs, 1, hd), f32(seqs, 1, hd),
@@ -701,29 +700,25 @@
             f32(TWO, QUAD, TWO, OCT, width), f32(TWO, QUAD, OCT, width), bf16(TWO, TWO, QUAD, OCT, width), bf16(LANES, width), bf16(QUAD, rest, width),
             f32(TWO, HALF, tail_w), f32(TWO, HALF, tail_w), f32(TWO, HALF, tail_w), f32(TWO, HALF, tail_w), f32(LANES, tail_w), f32(LANES, tail_w),
             f32(LANES, LANES), f32(LANES, LANES), f32(QUAD, OCT, LANES), f32(TWO, QUAD, OCT, LANES), f32(OCT, OCT, LANES),
-            dma(3), dma(full + TWO), dma(RING, TWO), dma(TWO), dma(QUAD), dma(KVS), dma(KVS), dma(steps), dma(steps), dma(TWO, steps // TWO), dma(TWO, steps // TWO),
-            dma(TWO, TWO), dma(TWO, TWO), dma(TWO, TWO), dma(TWO, TWO), dma(3), dma(3),
+            dma(3), dma(RING, TWO), dma(TWO), dma(QUAD), dma(KVS), dma(KVS), dma(steps), dma(steps), dma(TWO, steps // TWO), dma(TWO, steps // TWO),
+            dma(TWO, TWO), dma(TWO, TWO), dma(TWO, TWO), dma(TWO, TWO), dma(TWO, 3), dma(TWO, 3),
             dma(TWO, 3), dma(TWO, 3), dma(TWO), dma(TWO), dma(TWO), dma(TWO), dma(3), dma(3), dma(TWO, 3), dma(TWO, 3),
             dma(TWO, full), dma(TWO, full), dma(TWO, full), dma(TWO, full), dma(full), dma(full),
             dma(TWO), dma(TWO), dma(TWO), dma(TWO), dma(1), dma(1), dma(7), dma(7)],
-        compiler_params=pltpu.CompilerParams(collective_id=0, has_side_effects=True, vmem_limit_bytes=63 * TWO**20),
+        compiler_params=pltpu.CompilerParams(collective_id=0, has_side_effects=True, vmem_limit_bytes=VLIM),
     )(lens, hid, gain, gain_f, freq, wq, wk, wv, wg, wu, wo, wd, emb, k_cache, v_cache)
 
 
-def close_kernel(z_in, lse, kv, out, k_out, v_out, lse_out, buf, in_sem, out_sem):
+def close_kernel(z, lse, kv, out, k_out, v_out, lse_out, buf, out_sem):
     parts = buf.shape[0]
     rows = buf.shape[1]
-    loads = [pltpu.make_async_copy(z_in.at[pl.ds(i * rows, rows)], buf.at[i], in_sem.at[i]) for i in range(parts)]
     stores = [pltpu.make_async_copy(buf.at[i], out.at[pl.ds(i * rows, rows)], out_sem.at[i]) for i in range(parts)]
-    for load in loads:
-        load.start()
+    for i in range(parts):
+        buf[i] = z[i * rows:(i + 1) * rows, :] - lse[...]
+        stores[i].start()
     k_out[...] = kv[0]
     v_out[...] = kv[1]
     lse_out[...] = lse[...]
-    for i in range(parts):
-        loads[i].wait()
-        buf[i] = buf[i] - lse[...]
-        stores[i].start()
     for store in stores:
         store.wait()
 
@@ -737,10 +732,9 @@
     return pl.pallas_call(
         close_kernel, name="close",
         out_shape=[jax.ShapeDtypeStruct((share, rows), F32), small, small, jax.ShapeDtypeStruct((1, rows), F32)],
-        in_specs=[hbm, vmem, vmem], out_specs=[hbm, vmem, vmem, vmem],
-        scratch_shapes=[pltpu.VMEM((parts, share // parts, rows), F32),
-                        pltpu.SemaphoreType.DMA((parts,)), pltpu.SemaphoreType.DMA((parts,))],
-        compiler_params=pltpu.CompilerParams(vmem_limit_bytes=63 * 2**20),
+        in_specs=[vmem] * 3, out_specs=[hbm, vmem, vmem, vmem],
+        scratch_shapes=[pltpu.VMEM((parts, share // parts, rows), F32), pltpu.SemaphoreType.DMA((parts,))],
+        compiler_params=pltpu.CompilerParams(vmem_limit_bytes=16 * 2**20),
     )(z, lse, kv)
 
 

time: 164 us -> 160 us (0.976)
  Pallas kernels: 162 us -> 159 us
    pallas_call x1, Pallas kernels: 158 us -> 156 us  [step_call(): pl.pallas_call(step_kernel, name='step', out_shape=[bf16(TWO, OWN, hd), f...]
    pallas_call x1, Pallas kernels: 4.25 us -> 2.37 us  [close_call(): pl.pallas_call(close_kernel, name='close', out_shape=[jax.ShapeDtypeStruc...]
where the time goes in v5:
time: 160 us
  Pallas kernels  159 us (99%)
    pallas_call x1, Pallas kernels, step_call(): pl.pallas_call(step_kernel, name='step', out_shape=[bf16(TWO, OWN, hd), f...  156 us

profile of v5, /device:TPU:0, one launch (start us, length us, event | category | flops | bytes accessed | tf_op | source)
XLA Modules:
  0.0 159.9 jit_solution(2676004774743041599)
XLA Ops:
  0.6 0.5 fusion.4.freq
  1.2 156.3 %step.1 = (bf16[2,16,128]{2,1,0:T(8,128)(2,1)S(1)}, f32[6304,128]{1,0:T(8,128)S(1)}, f32[1,128]{1,0:T(1,128)S(1)}) custom-call(s32[128]{0:T(128)} %lens.1, bf16[8,16,1024]{2,1,0:T(8,128)(2,1)} %bitcast.5, f32[1,1024]{1,0:T(1,128)} %bitcast.6, f32[1,1024]{1,0:T(1,128)} %bitcast.7, f32[1,128]{1,0:T(1,128)} %fusion.4.freq, bf16[1024,2048]{1,0:T(8,128)(2,1)} %wq.1, ...), custom_call_target="tpu_custom_call" | custom-call | tf_op jit(solution)/shard_map/step/pallas_call | solution.py:688
  157.5 2.4 %close.1 = (f32[6304,128]{1,0:T(8,128)}, bf16[16,128]{1,0:T(8,128)(2,1)}, bf16[16,128]{1,0:T(8,128)(2,1)}, f32[1,128]{1,0:T(1,128)}) custom-call(f32[6304,128]{1,0:T(8,128)S(1)} %get-tuple-element.11.z, f32[1,128]{1,0:T(1,128)S(1)} %get-tuple-element.12.lse, bf16[2,16,128]{2,1,0:T(8,128)(2,1)S(1)} %get-tuple-element.13.kv), custom_call_target="tpu_custom_call" | custom-call | tf_op jit(solution)/shard_map/close/pallas_call | solution.py:732

commit v6 on v5

--- a/solution.py
+++ b/solution.py
@@ -51,23 +51,21 @@
     return tile[:, 0:1], tile[:, 1:2]
 
 
-def norm_stats(values, stat, y, xi, send_sems, recv_sems, ready, size, after=lambda: None):
-    rows, width = values.shape
-    mean_own = jnp.sum(values, axis=1, keepdims=True) / width
+def stat_hops(stat, y, xi, send_sems, recv_sems):
+    return [send(stat.at[xi], stat.at[xi], send_sems.at[d - 1], recv_sems.at[d - 1], y, (xi + d) % 4) for d in range(1, 4)]
+
+
+def put_stats(values, stat, xi):
+    mean_own = jnp.sum(values, axis=1, keepdims=True) / values.shape[1]
     diff = values - mean_own
     stat[xi] = to_lanes(mean_own, jnp.sum(diff * diff, axis=1, keepdims=True))
-    ready()
-    copies = [send(stat.at[xi], stat.at[xi], send_sems.at[d - 1], recv_sems.at[d - 1], y, (xi + d) % size)
-              for d in range(1, size)]
-    for copy in copies:
-        copy.start()
-    after()
-    for copy in copies:
-        copy.wait()
-    tiles = [stat[i] for i in range(size)]
-    mean_all = sum(t[0:1] for t in tiles) / size
-    spread = sum(t[1:TWO] for t in tiles) + width * sum((t[0:1] - mean_all) * (t[0:1] - mean_all) for t in tiles)
-    mean_col, rstd_col = to_columns(mean_all, lax.rsqrt(spread / (width * size) + EPS))
+
+
+def take_stats(stat, rows, share):
+    tiles = [stat[i] for i in range(4)]
+    mean_all = sum(t[0:1] for t in tiles) / 4
+    spread = sum(t[1:2] for t in tiles) + share * sum((t[0:1] - mean_all) * (t[0:1] - mean_all) for t in tiles)
+    mean_col, rstd_col = to_columns(mean_all, lax.rsqrt(spread / (share * 4) + EPS))
     return mean_col[:rows], rstd_col[:rows]
 
 
@@ -76,13 +74,13 @@
 RING = 6
 KVS = 3
 VLIM = 121 * 2**19
-HELD = 6
+HELD = 7
 
 
 def step_kernel(lens, hid_h, gain_h, gain_fh, freq, wq, wk, wv, wg, wu, wo, wd, emb, k_hbm, v_hbm,
                 kv_out, z_out, lse_out,
                 hid, gain, gain_f, cos, sin, n_perm, ring, w_kv, part_q, ga_q, sb_q, gb_q, total, q_rot, q_full, q_heads, o_heads, kn, vn,
-                pool, act, o_in, o_all, k_buf, v_buf, scores, probs, acc, y_got, f_all, f_nat, e_tail,
+                pool, act, o_in, o_all, k_buf, v_buf, scores, probs, acc, y_got, r_buf, f_all, f_nat, e_tail,
                 t_a, t_b, tg_a, tg_b, t_c, tg_c, top, mass_l, stat, stat_f, stat_z,
                 i_sem, r_sem, kv_sem, tail_sem, k_sem, v_sem, a_s, a_r, b_s, b_r, m_s, m_r, p_s, p_r, q_s, q_r,
                 o_s, o_r, y_s, y_r, f_s, f_r, st_s, st_r, sf_s, sf_r,
@@ -233,7 +231,13 @@
     for load in inputs:
         load.wait()
     h = hid[...].astype(F32).reshape(LANES, width)
-    mean, rstd = norm_stats(h, stat, y, xi, st_s, st_r, ready, 4)
+    put_stats(h, stat, xi)
+    ready()
+    first = stat_hops(stat, y, xi, st_s, st_r)
+    start(first)
+    for copy in first:
+        copy.wait()
+    mean, rstd = take_stats(stat, LANES, width)
     normed = ((h - mean) * rstd * gain[...]).astype(BF16)
     for hf in range(TWO):
         for core_o in range(TWO):
@@ -426,15 +430,21 @@
 
         lax.fori_loop(0, no, from_heads, 0)
 
-    def finish_layer(hf, after):
+    def finish_sum(hf):
         hop_y(hf).wait_recv()
-        res = [hid[y * 4 + (i % TWO) * TWO + i // TWO, hf * 8:hf * 8 + 8].astype(F32) for i in range(4)]
+        res = [hid[y * 4 + (i % 2) * 2 + i // 2, hf * 8:hf * 8 + 8].astype(F32) for i in range(4)]
         branch = acc[hf, :, y] + y_got[hf]
-        r = jnp.concatenate(res, axis=0) + branch.reshape(PAIR, width)
-        mean, rstd = norm_stats(r, stat_f.at[hf], y, xi, sf_s.at[hf], sf_r.at[hf], lambda: None, 4, after)
-        f = ((r - mean) * rstd * gain_f[...]).astype(BF16)
+        r_buf[...] = jnp.concatenate(res, axis=0) + branch.reshape(PAIR, width)
+        put_stats(r_buf[...], stat_f.at[hf], xi)
+        start(stat_hops(stat_f.at[hf], y, xi, sf_s.at[hf], sf_r.at[hf]))
+
+    def finish_norm(hf):
+        for copy in stat_hops(stat_f.at[hf], y, xi, sf_s.at[hf], sf_r.at[hf]):
+            copy.wait()
+        mean, rstd = take_stats(stat_f.at[hf], PAIR, width)
+        f = ((r_buf[...] - mean) * rstd * gain_f[...]).astype(BF16)
         for i in range(4):
-            f_all[hf, y, (i % TWO) * TWO + i // TWO] = f[i * 8:(i + 1) * 8]
+            f_all[hf, y, (i % 2) * 2 + i // 2] = f[i * 8:(i + 1) * 8]
         hop_f(hf).start()
 
     def each(body, low, high):
@@ -458,10 +468,12 @@
         attend(i)
         pl.when(i < 8)(lambda: activate(0, i))
 
+        pl.when((i == 5) | (i == 7))(lambda: hop_b(1, (i - 5) // 2).start())
+
         @pl.when(i == 8)
         def _():
             pass_o(0, 0)
-            each(lambda p: hop_b(1, p).start(), 0, HELD)
+            each(lambda p: hop_b(1, p).start(), 2, HELD)
 
         pl.when(i == 10)(lambda: pass_m(0))
         pl.when(i == 11)(lambda: pass_o(0, 1))
@@ -472,16 +484,22 @@
             each(lambda p: hop_b(0, p).wait_send(), 0, 8)
             contract(0)
             hop_y(0).start()
-            each(lambda p: activate(1, p), 0, TWO)
+            each(lambda p: activate(1, p), 0, 2)
 
         @pl.when(i == 13)
         def _():
-            finish_layer(0, lambda: each(lambda p: hop_b(1, p).start(), HELD, 8))
+            finish_sum(0)
+            each(lambda p: hop_b(1, p).start(), HELD, 8)
+
+        @pl.when(i == 14)
+        def _():
+            finish_norm(0)
+            each(lambda p: activate(1, p), 2, 4)
 
     each(mix, 0, seqs)
+    each(lambda p: activate(1, p), 4, 8)
     hop_f(0).wait_recv()
     send_heads(1)
-    each(lambda p: activate(1, p), TWO, 4)
 
     def out_at(hf, k):
         return 56 - hf * 6 + k
@@ -536,10 +554,7 @@
             if hf == 0:
                 pl.when(k < full - TWO)(lambda: lhop_b(0, k).start())
 
-                @pl.when(k == 0)
-                def _():
-                    each(lambda p: activate(1, p), 4, 8)
-                    pass_o(1, 0)
+                pl.when(k == 0)(lambda: pass_o(1, 0))
             else:
                 lhop_b(1, k).start()
 
@@ -556,17 +571,16 @@
         if hf == 1:
             thop_b(1).start()
 
-    def release():
-        each(lambda k: lhop_b(0, k).start(), full - TWO, full)
-        thop_b(0).start()
-
     outward(0)
     pass_m(1)
     pass_o(1, 1)
     each(lambda p: hop_b(1, p).wait_send(), 0, 8)
     contract(1)
     hop_y(1).start()
-    finish_layer(1, release)
+    finish_sum(1)
+    each(lambda k: lhop_b(0, k).start(), full - 2, full)
+    thop_b(0).start()
+    finish_norm(1)
     hop_f(1).wait_recv()
     outward(1)
 
@@ -697,7 +711,7 @@
             f32(QUAD * steps, TWO, TWO, OWN, TWO * FC), bf16(TWO, TWO, TWO, TWO, OWN, steps // TWO * FC),
             bf16(TWO, TWO, OCT, qc), bf16(TWO, TWO, TWO, TWO, OCT, qc),
             bf16(KVS, length, hd), bf16(KVS, length, hd), f32(heads, length), bf16(heads, length),
-            f32(TWO, QUAD, TWO, OCT, width), f32(TWO, QUAD, OCT, width), bf16(TWO, TWO, QUAD, OCT, width), bf16(LANES, width), bf16(QUAD, rest, width),
+            f32(TWO, QUAD, TWO, OCT, width), f32(TWO, QUAD, OCT, width), f32(PAIR, width), bf16(TWO, TWO, QUAD, OCT, width), bf16(LANES, width), bf16(QUAD, rest, width),
             f32(TWO, HALF, tail_w), f32(TWO, HALF, tail_w), f32(TWO, HALF, tail_w), f32(TWO, HALF, tail_w), f32(LANES, tail_w), f32(LANES, tail_w),
             f32(LANES, LANES), f32(LANES, LANES), f32(QUAD, OCT, LANES), f32(TWO, QUAD, OCT, LANES), f32(OCT, OCT, LANES),
             dma(3), dma(RING, TWO), dma(TWO), dma(QUAD), dma(KVS), dma(KVS), dma(steps), dma(steps), dma(TWO, steps // TWO), dma(TWO, steps // TWO),

time: 160 us -> 160 us (level)
  no operation moved by 1% of the time
where the time goes in v6:
time: 160 us
  Pallas kernels  159 us (99%)
    pallas_call x1, Pallas kernels, step_call(): pl.pallas_call(step_kernel, name='step', out_shape=[bf16(TWO, OWN, hd), f...  156 us

profile of v6, /device:TPU:0, one launch (start us, length us, event | category | flops | bytes accessed | tf_op | source)
XLA Modules:
  0.0 159.7 jit_solution(15948454267963001081)
XLA Ops:
  0.6 0.5 fusion.4.freq
  1.2 156.2 %step.1 = (bf16[2,16,128]{2,1,0:T(8,128)(2,1)S(1)}, f32[6304,128]{1,0:T(8,128)S(1)}, f32[1,128]{1,0:T(1,128)S(1)}) custom-call(s32[128]{0:T(128)} %lens.1, bf16[8,16,1024]{2,1,0:T(8,128)(2,1)} %bitcast.5, f32[1,1024]{1,0:T(1,128)} %bitcast.6, f32[1,1024]{1,0:T(1,128)} %bitcast.7, f32[1,128]{1,0:T(1,128)} %fusion.4.freq, bf16[1024,2048]{1,0:T(8,128)(2,1)} %wq.1, ...), custom_call_target="tpu_custom_call" | custom-call | tf_op jit(solution)/shard_map/step/pallas_call | solution.py:702
  157.3 2.4 %close.1 = (f32[6304,128]{1,0:T(8,128)}, bf16[16,128]{1,0:T(8,128)(2,1)}, bf16[16,128]{1,0:T(8,128)(2,1)}, f32[1,128]{1,0:T(1,128)}) custom-call(f32[6304,128]{1,0:T(8,128)S(1)} %get-tuple-element.11.z, f32[1,128]{1,0:T(1,128)S(1)} %get-tuple-element.12.lse, bf16[2,16,128]{2,1,0:T(8,128)(2,1)S(1)} %get-tuple-element.13.kv), custom_call_target="tpu_custom_call" | custom-call | tf_op jit(solution)/shard_map/close/pallas_call | solution.py:746

commit v7 on v6

--- a/solution.py
+++ b/solution.py
@@ -81,7 +81,7 @@
                 kv_out, z_out, lse_out,
                 hid, gain, gain_f, cos, sin, n_perm, ring, w_kv, part_q, ga_q, sb_q, gb_q, total, q_rot, q_full, q_heads, o_heads, kn, vn,
                 pool, act, o_in, o_all, k_buf, v_buf, scores, probs, acc, y_got, r_buf, f_all, f_nat, e_tail,
-                t_a, t_b, tg_a, tg_b, t_c, tg_c, top, mass_l, stat, stat_f, stat_z,
+                t_a, t_b, t_x, tg_a, tg_b, t_c, tg_c, top, mass_l, stat, stat_f, stat_z,
                 i_sem, r_sem, kv_sem, tail_sem, k_sem, v_sem, a_s, a_r, b_s, b_r, m_s, m_r, p_s, p_r, q_s, q_r,
                 o_s, o_r, y_s, y_r, f_s, f_r, st_s, st_r, sf_s, sf_r,
                 la_s, la_r, lb_s, lb_r, lc_s, lc_r, ta_s, ta_r, tb_s, tb_r, tc_s, tc_r, sz_s, sz_r):
@@ -116,6 +116,8 @@
         return [pltpu.make_async_copy(w.at[:, cols], ring.at[slot, i], r_sem.at[slot, i]) for i, w in enumerate((wg, wu))]
 
     kv_w = [pltpu.make_async_copy(w, w_kv.at[:, pl.ds(i * hd, hd)], kv_sem.at[i]) for i, w in enumerate((wk, wv))]
+    for load in inputs:
+        load.wait()
     start(q_loads(0))
     start(q_loads(1))
     start(kv_w)
@@ -228,8 +230,6 @@
         lane = lax.broadcasted_iota(jnp.int32, (OWN, hd), 1)
         return jnp.cos(angle), jnp.where(lane < hd // TWO, -jnp.sin(angle), jnp.sin(angle))
 
-    for load in inputs:
-        load.wait()
     h = hid[...].astype(F32).reshape(LANES, width)
     put_stats(h, stat, xi)
     ready()
@@ -520,7 +520,7 @@
         return send(t_a.at[hf], tg_a.at[hf], ta_s.at[hf], ta_r.at[hf], y, partner)
 
     def thop_b(hf):
-        return send(t_b.at[hf], tg_b.at[hf], tb_s.at[hf], tb_r.at[hf], y, twin)
+        return send(t_x.at[hf], tg_b.at[hf], tb_s.at[hf], tb_r.at[hf], y, twin)
 
     thop_c = send(t_c, tg_c, tc_s.at[0], tc_r.at[0], y, partner)
     nt = (((1,), (1,)), ((), ()))
@@ -567,7 +567,10 @@
         thop_a(hf).start()
         t_b[hf, :, :rest] = tail_product(left, 1)
         thop_a(hf).wait_recv()
-        t_b[hf] += tg_a[hf]
+        both = t_b[hf] + tg_a[hf]
+        t_x[hf, :HALF] = both[:, :LANES]
+        quarters = [both[i * OWN:(i + 1) * OWN, LANES:rest] for i in range(QUAD)]
+        t_x[hf, HALF:] = jnp.concatenate(quarters, axis=1)
         if hf == 1:
             thop_b(1).start()
 
@@ -635,7 +638,13 @@
     each(finish, 0, full)
     thop_b(0).wait_recv()
     thop_b(1).wait_recv()
-    z_tail = tg_c[...] + weave(tg_b[0], tg_b[1])
+    over = rest - LANES
+
+    def unpack(block):
+        edge = jnp.concatenate([block[HALF:, i * over:(i + 1) * over] for i in range(QUAD)], axis=0)
+        return jnp.concatenate([block[:HALF], edge, jnp.zeros((HALF, LANES - over), F32)], axis=1)
+
+    z_tail = tg_c[...] + weave(unpack(tg_b[0]), unpack(tg_b[1]))
     lane = lax.broadcasted_iota(jnp.int32, z_tail.shape, 1)
     fold(jnp.where(lane < rest, z_tail, LOW))
     z_out[full * WB:, :] = z_tail.T[:rest]
@@ -712,7 +721,7 @@
             bf16(TWO, TWO, OCT, qc), bf16(TWO, TWO, TWO, TWO, OCT, qc),
             bf16(KVS, length, hd), bf16(KVS, length, hd), f32(heads, length), bf16(heads, length),
             f32(TWO, QUAD, TWO, OCT, width), f32(TWO, QUAD, OCT, width), f32(PAIR, width), bf16(TWO, TWO, QUAD, OCT, width), bf16(LANES, width), bf16(QUAD, rest, width),
-            f32(TWO, HALF, tail_w), f32(TWO, HALF, tail_w), f32(TWO, HALF, tail_w), f32(TWO, HALF, tail_w), f32(LANES, tail_w), f32(LANES, tail_w),
+            f32(TWO, HALF, tail_w), f32(TWO, HALF, tail_w), f32(TWO, HALF + OWN, LANES), f32(TWO, HALF, tail_w), f32(TWO, HALF + OWN, LANES), f32(LANES, tail_w), f32(LANES, tail_w),
             f32(LANES, LANES), f32(LANES, LANES), f32(QUAD, OCT, LANES), f32(TWO, QUAD, OCT, LANES), f32(OCT, OCT, LANES),
             dma(3), dma(RING, TWO), dma(TWO), dma(QUAD), dma(KVS), dma(KVS), dma(steps), dma(steps), dma(TWO, steps // TWO), dma(TWO, steps // TWO),
             dma(TWO, TWO), dma(TWO, TWO), dma(TWO, TWO), dma(TWO, TWO), dma(TWO, 3), dma(TWO, 3),

time: 160 us -> 156 us (0.975)
  Pallas kernels: 159 us -> 155 us
    pallas_call x1, Pallas kernels: 156 us -> 153 us  [step_call(): pl.pallas_call(step_kernel, name='step', out_shape=[bf16(TWO, OWN, hd), f...]
where the time goes in v7:
time: 156 us
  Pallas kernels  155 us (99%)
    pallas_call x1, Pallas kernels, step_call(): pl.pallas_call(step_kernel, name='step', out_shape=[bf16(TWO, OWN, hd), f...  153 us

profile of v7, /device:TPU:0, one launch (start us, length us, event | category | flops | bytes accessed | tf_op | source)
XLA Modules:
  0.0 156.2 jit_solution(17042858910177660067)
XLA Ops:
  0.6 0.5 fusion.4.freq
  1.2 152.6 %step.1 = (bf16[2,16,128]{2,1,0:T(8,128)(2,1)S(1)}, f32[6304,128]{1,0:T(8,128)S(1)}, f32[1,128]{1,0:T(1,128)S(1)}) custom-call(s32[128]{0:T(128)} %lens.1, bf16[8,16,1024]{2,1,0:T(8,128)(2,1)} %bitcast.5, f32[1,1024]{1,0:T(1,128)} %bitcast.6, f32[1,1024]{1,0:T(1,128)} %bitcast.7, f32[1,128]{1,0:T(1,128)} %fusion.4.freq, bf16[1024,2048]{1,0:T(8,128)(2,1)} %wq.1, ...), custom_call_target="tpu_custom_call" | custom-call | tf_op jit(solution)/shard_map/step/pallas_call | solution.py:711
  153.8 2.4 %close.1 = (f32[6304,128]{1,0:T(8,128)}, bf16[16,128]{1,0:T(8,128)(2,1)}, bf16[16,128]{1,0:T(8,128)(2,1)}, f32[1,128]{1,0:T(1,128)}) custom-call(f32[6304,128]{1,0:T(8,128)S(1)} %get-tuple-element.11.z, f32[1,128]{1,0:T(1,128)S(1)} %get-tuple-element.12.lse, bf16[2,16,128]{2,1,0:T(8,128)(2,1)S(1)} %get-tuple-element.13.kv), custom_call_target="tpu_custom_call" | custom-call | tf_op jit(solution)/shard_map/close/pallas_call | solution.py:755

commit v8 on v7

--- a/solution.py
+++ b/solution.py
@@ -77,7 +77,7 @@
 HELD = 7
 
 
-def step_kernel(lens, hid_h, gain_h, gain_fh, freq, wq, wk, wv, wg, wu, wo, wd, emb, k_hbm, v_hbm,
+def step_kernel(lens, hid_h, gain_h, gain_fh, wq, wk, wv, wg, wu, wo, wd, emb, k_hbm, v_hbm,
                 kv_out, z_out, lse_out,
                 hid, gain, gain_f, cos, sin, n_perm, ring, w_kv, part_q, ga_q, sb_q, gb_q, total, q_rot, q_full, q_heads, o_heads, kn, vn,
                 pool, act, o_in, o_all, k_buf, v_buf, scores, probs, acc, y_got, r_buf, f_all, f_nat, e_tail,
@@ -226,8 +226,8 @@
     def turns(owner):
         row = lax.broadcasted_iota(jnp.int32, (OWN, hd), 0)
         pos = functools.reduce(lambda acc_, r: jnp.where(row == r, lens[owner * OWN + r], acc_), range(OWN), jnp.zeros((OWN, hd), jnp.int32))
-        angle = pos.astype(F32) * freq[...]
         lane = lax.broadcasted_iota(jnp.int32, (OWN, hd), 1)
+        angle = pos.astype(F32) * ROPE_BASE ** (-((lane % (hd // 2)).astype(F32) * 2.0) / hd)
         return jnp.cos(angle), jnp.where(lane < hd // TWO, -jnp.sin(angle), jnp.sin(angle))
 
     h = hid[...].astype(F32).reshape(LANES, width)
@@ -685,7 +685,7 @@
         hop.wait_send()
 
 
-def step_call(lens, hid, gain, gain_f, freq, wq, wk, wv, wg, wu, wo, wd, emb, k_cache, v_cache):
+def step_call(lens, hid, gain, gain_f, wq, wk, wv, wg, wu, wo, wd, emb, k_cache, v_cache):
     width = hid.shape[TWO]
     qc, hd = wq.shape[1], wk.shape[1]
     seqs, length, _ = k_cache.shape
@@ -711,7 +711,7 @@
     return pl.pallas_call(
         step_kernel, name="step",
         out_shape=[bf16(TWO, OWN, hd), f32(share, LANES), f32(1, LANES)],
-        in_specs=[pl.BlockSpec(memory_space=pltpu.SMEM)] + [hbm] * 3 + [vmem] + [hbm] * 10, out_specs=[vmem] * 3,
+        in_specs=[pl.BlockSpec(memory_space=pltpu.SMEM)] + [hbm] * 13, out_specs=[vmem] * 3,
         scratch_shapes=[
             bf16(OCT, OWN, width), f32(1, width), f32(1, width), f32(TWO, OWN, hd), f32(TWO, OWN, hd),
             bf16(LANES, width), bf16(RING, TWO, width, FC), bf16(width, TWO * hd),
@@ -729,7 +729,7 @@
             dma(TWO, full), dma(TWO, full), dma(TWO, full), dma(TWO, full), dma(full), dma(full),
             dma(TWO), dma(TWO), dma(TWO), dma(TWO), dma(1), dma(1), dma(7), dma(7)],
         compiler_params=pltpu.CompilerParams(collective_id=0, has_side_effects=True, vmem_limit_bytes=VLIM),
-    )(lens, hid, gain, gain_f, freq, wq, wk, wv, wg, wu, wo, wd, emb, k_cache, v_cache)
+    )(lens, hid, gain, gain_f, wq, wk, wv, wg, wu, wo, wd, emb, k_cache, v_cache)
 
 
 def close_kernel(z, lse, kv, out, k_out, v_out, lse_out, buf, out_sem):
@@ -767,12 +767,9 @@
     def local_step(hidden, cache_len, k_cache, v_cache, g_attn, w_query, w_key, w_value,
                    w_gate, w_up, w_out, w_down, g_final, embedding):
         width = hidden.shape[1]
-        own_rows, _, head_dim = k_cache.shape
-        half = head_dim // TWO
-        lane = jnp.arange(head_dim)
-        inv_freq = ROPE_BASE ** (-((lane % half).astype(F32) * 2.0) / head_dim)
+        own_rows = k_cache.shape[0]
         kv_new, logits_t, log_norm = step_call(
-            cache_len, hidden.reshape(8, own_rows, width), g_attn[None], g_final[None], inv_freq[None],
+            cache_len, hidden.reshape(8, own_rows, width), g_attn[None], g_final[None],
             w_query, w_key, w_value, w_gate, w_up, w_out, w_down, embedding, k_cache, v_cache)
         log_probs, key_own, value_own, log_norm = close_call(logits_t, log_norm, kv_new)
         return key_own, value_own, log_probs.T, log_norm[0]

time: 156 us -> 156 us (level)
  no operation moved by 1% of the time
where the time goes in v8:
time: 156 us
  Pallas kernels  155 us (99%)
    pallas_call x1, Pallas kernels, step_call(): pl.pallas_call(step_kernel, name='step', out_shape=[bf16(TWO, OWN, hd), f...  153 us

profile of v8, /device:TPU:0, one launch (start us, length us, event | category | flops | bytes accessed | tf_op | source)
XLA Modules:
  0.0 155.5 jit_solution(16075998216406149384)
XLA Ops:
  0.6 152.5 %step.1 = (bf16[2,16,128]{2,1,0:T(8,128)(2,1)S(1)}, f32[6304,128]{1,0:T(8,128)S(1)}, f32[1,128]{1,0:T(1,128)S(1)}) custom-call(s32[128]{0:T(128)} %lens.1, bf16[8,16,1024]{2,1,0:T(8,128)(2,1)} %bitcast.5, f32[1,1024]{1,0:T(1,128)} %bitcast.6, f32[1,1024]{1,0:T(1,128)} %bitcast.7, bf16[1024,2048]{1,0:T(8,128)(2,1)} %wq.1, bf16[1024,128]{1,0:T(8,128)(2,1)} %wk.1, ...), custom_call_target="tpu_custom_call" | custom-call | tf_op jit(solution)/shard_map/step/pallas_call | solution.py:711
  153.2 2.4 %close.1 = (f32[6304,128]{1,0:T(8,128)}, bf16[16,128]{1,0:T(8,128)(2,1)}, bf16[16,128]{1,0:T(8,128)(2,1)}, f32[1,128]{1,0:T(1,128)}) custom-call(f32[6304,128]{1,0:T(8,128)S(1)} %get-tuple-element.11.z, f32[1,128]{1,0:T(1,128)S(1)} %get-tuple-element.12.lse, bf16[2,16,128]{2,1,0:T(8,128)(2,1)S(1)} %get-tuple-element.13.kv), custom_call_target="tpu_custom_call" | custom-call | tf_op jit(solution)/shard_map/close/pallas_call | solution.py:755
